TPU v7x, 32 devices: a whole 2x2x4 slice. The times are simulated.
32 devices in a mesh: dp: 8 (over z, x), row: 2 (over core), col: 2 (over y).
Axes of the slice: x: 2, y: 2, z: 4, core: 2. Of those that a mesh axis runs over, the one named last changes fastest.
Arguments:
- tokens: bfloat16 [8, 2048, 768], P('dp', 'col', 'row'), may hold values from -7 to 7
- cotangent: bfloat16 [8, 2048, 768], P('dp', 'col', 'row'), may hold values from -6 to 6
- segments: int32 [8, 2048], P('dp', 'row'), may hold values from 0 to 3, never falling along the last dimension, each value on 1 to 1024 neighbouring positions
- valid: int32 [8, 2048], P('dp', 'col'), may hold values 0 or 1
- w_query: bfloat16 [2, 768, 768], P(None, 'row', 'col'), may hold values from -0.21875 to 0.21875
- w_key: bfloat16 [2, 768, 768], P(None, 'row', 'col'), may hold values from -0.21875 to 0.21875
- w_value: bfloat16 [2, 768, 768], P(None, 'row', 'col'), may hold values from -0.21875 to 0.21875
- w_out: bfloat16 [2, 768, 768], P(None, 'col', 'row'), may hold values from -3.5 to 3.5
- w_up: bfloat16 [2, 768, 3072], P(None, 'row', 'col'), may hold values from -0.21875 to 0.21875
- w_down: bfloat16 [2, 3072, 768], P(None, 'col', 'row'), may hold values from -0.109375 to 0.109375
- vectors: float32 [2, 9216], replicated, may hold values from -2 to 2, as said below
- vector_m: float32 [2, 9216], replicated, may hold values from -224 to 224
- vector_v: float32 [2, 9216], replicated, may hold values from 163.84 to 16384
- tile_order: int32 [2, 2, 216], P('row', 'col'), may hold values from 0 to 215, each once within a row
- basis_left: float32 [2, 2, 216, 128, 128], P('row', 'col', 'dp'), may hold values from -0.5 to 0.5
- basis_right: float32 [2, 2, 216, 128, 128], P('row', 'col', 'dp'), may hold values from -0.5 to 0.5
- tile_m: float32 [2, 2, 216, 128, 128], P('row', 'col', 'dp'), may hold values from -224 to 224
- tile_v: float32 [2, 2, 216, 128, 128], P('row', 'col', 'dp'), may hold values from 163.84 to 16384
Outputs:
- final_out: bfloat16 [8, 2048, 768], P('dp', 'col', 'row')
- grad_tokens: float32 [8, 2048, 768], P('dp', 'col', 'row')
- statistics: float32 [2], replicated
- vector_grad: float32 [2, 9216], replicated
- vector_m_new: float32 [2, 9216], replicated
- vector_v_new: float32 [2, 9216], replicated
- vector_update: float32 [2, 9216], replicated
- tile_grad: float32 [2, 2, 216, 128, 128], P('row', 'col', 'dp')
- tile_m_new: float32 [2, 2, 216, 128, 128], P('row', 'col', 'dp')
- tile_v_new: float32 [2, 2, 216, 128, 128], P('row', 'col', 'dp')
- tile_update: float32 [2, 2, 216, 128, 128], P('row', 'col', 'dp')
Inputs may be any that keep to these rules, and one draw needn't show every extreme that they name: `segments`: each sequence's ids start at 0 and rise by one from document to document. `tile_order`: each row (r, c) names every code once, so every owner takes at most 27 tiles and owner 0 takes 27. `vectors`: gains lie in 0.1 to 1.9.
All inputs are finite; a program needn't handle non-finite values. No bound on the sum of `valid` on one device may be relied on, other than what follows from the above.
Results may differ from a plain program's by a relative error of at most 0.022.
Values may be sent and summed in bfloat16 or wider, within the bound.
A program may use at most 384 MiB of HBM per device.

v0:
```python
import jax
import jax.numpy as jnp
from jax import lax
from jax.sharding import PartitionSpec as P

D = 768
DH = 64
LAYERS = 2
HALF = 512
QBLK = 512
TILE = 128


HIGHEST = lax.Precision.HIGHEST
NEG_BIG = -1e30
NORM_EPS = 1e-06
ADAM_EPS = 1e-08
TILE_RATE = 0.03
VECTOR_RATE = 0.1
DECAY = 0.5


def with_halo(block, sides, width):
    for axis, dim in sides:
        count = lax.axis_size(axis)
        forward = [(i, i + 1) for i in range(count - 1)]
        backward = [(target, source) for source, target in forward]
        low = lax.ppermute(
            lax.slice_in_dim(block, block.shape[dim] - width, None, axis=dim), axis, forward
        )
        high = lax.ppermute(lax.slice_in_dim(block, 0, width, axis=dim), axis, backward)
        block = jnp.concatenate([low, block, high], axis=dim)
    return block


def matmul(left_mat, right_mat):
    return jnp.dot(left_mat, right_mat, preferred_element_type=jnp.float32)


def matmul_bt(left_mat, right_mat):
    return lax.dot_general(
        left_mat, right_mat, (((1,), (1,)), ((), ())), preferred_element_type=jnp.float32
    )


def matmul_at(left_mat, right_mat):
    return lax.dot_general(
        left_mat, right_mat, (((0,), (0,)), ((), ())), preferred_element_type=jnp.float32
    )


def gather_cols(value):
    return lax.all_gather(value, "col", axis=0, tiled=True)


def gather_rows(value):
    return lax.all_gather(value, "row", axis=0, tiled=True)


def scatter_rows(full_rows, weight, transposed):
    return lax.psum_scatter(
        matmul_bt(full_rows, weight) if transposed else matmul(full_rows, weight),
        "row",
        scatter_dimension=0,
        tiled=True,
    )


def scatter_cols(full_rows, weight, transposed):
    return lax.psum_scatter(
        (matmul_bt(full_rows, weight) if transposed else matmul(full_rows, weight)).astype(
            jnp.bfloat16
        ),
        "col",
        scatter_dimension=0,
        tiled=True,
    ).astype(jnp.float32)


def row_totals(first_sum, second_sum):
    return lax.psum((first_sum, second_sum), "row")


def norm_forward(resid, gain_vec, shift_vec):
    total_sum, square_sum = row_totals(jnp.sum(resid, 1), jnp.sum(resid * resid, 1))
    row_mean = total_sum / D
    row_var = square_sum / D - row_mean * row_mean
    inv_std = lax.rsqrt(row_var + NORM_EPS)
    normed = (resid - row_mean[:, None]) * inv_std[:, None]
    return (normed * gain_vec + shift_vec, normed, inv_std)


def norm_backward(grad_in, normed, inv_std, gain_vec):
    d_normed = grad_in * gain_vec
    first_sum, second_sum = row_totals(jnp.sum(d_normed, 1), jnp.sum(d_normed * normed, 1))
    d_resid = inv_std[:, None] * (
        d_normed - first_sum[:, None] / D - normed * (second_sum[:, None] / D)
    )
    return (d_resid, jnp.sum(grad_in * normed, 0), jnp.sum(grad_in, 0))


def vector_offsets(d_row, hd_col, ff_col):
    row_idx = lax.axis_index("row")
    col_idx = lax.axis_index("col")
    spots = [(col_idx * hd_col, hd_col), (D + col_idx * hd_col, hd_col)]
    for spot in range(2, 8):
        spots.append((spot * D + row_idx * d_row, d_row))
    spots.append((8 * D + col_idx * ff_col, ff_col))
    return spots


def take_parts(vec_row, spots):
    return tuple(
        (lax.dynamic_slice_in_dim(vec_row, place_at, span_size, 0) for place_at, span_size in spots)
    )


def place_parts(pieces, spots, vec_len):
    placed = jnp.zeros((vec_len,), jnp.float32)
    for piece_vec, spot in zip(pieces, spots):
        placed = lax.dynamic_update_slice_in_dim(placed, piece_vec, spot[0], 0)
    return placed


def block_visible(seg_local, seg_ext, key_ok, offset, key_span):
    query_seg = seg_local[offset : offset + QBLK]
    key_seg = seg_ext[offset : offset + key_span]
    offset_gap = jnp.arange(QBLK)[:, None] + HALF - jnp.arange(key_span)[None, :]
    near_keys = jnp.abs(offset_gap) < HALF
    return (
        (query_seg[:, None] == key_seg[None, :])
        & near_keys
        & key_ok[offset : offset + key_span][None, :]
    )


def block_scores(query_rows, key_rows, visible):
    head_count = query_rows.shape[1] // DH
    query_heads = query_rows.reshape(query_rows.shape[0], head_count, DH)
    key_heads = key_rows.reshape(key_rows.shape[0], head_count, DH)
    raw_scores = jnp.einsum(
        "qhd,khd->hqk", query_heads, key_heads, preferred_element_type=jnp.float32
    ) * DH ** (-0.5)
    return (jnp.where(visible[None], raw_scores, NEG_BIG), query_heads, key_heads)


def block_tiles(block_mat):
    row_span, col_span = block_mat.shape
    return (
        block_mat.reshape(row_span // TILE, TILE, col_span // TILE, TILE)
        .transpose(0, 2, 1, 3)
        .reshape(-1, TILE, TILE)
    )


def gelu_exact(inner):
    return jax.nn.gelu(inner, approximate=False)


def layer_forward(hidden, weights, vec_row, seg_local, seg_ext, key_ok):
    w_query, w_key, w_value, w_out, w_up, w_down = weights
    hd_col = w_query.shape[1]
    spots = vector_offsets(hidden.shape[1], hd_col, w_up.shape[1])
    bias_q, bias_v, bias_o, bias_down, gain_one, shift_one, gain_two, shift_two, bias_up = (
        take_parts(vec_row, spots)
    )
    inputs_full = gather_cols(hidden.astype(jnp.bfloat16))
    w_qkv = jnp.concatenate((w_query, w_key, w_value), 1)
    projected = scatter_rows(inputs_full, w_qkv, False)
    queries = (projected[:, :hd_col] + bias_q).astype(jnp.bfloat16)
    kv_local = jnp.concatenate(
        (projected[:, hd_col : 2 * hd_col], projected[:, 2 * hd_col :] + bias_v), 1
    ).astype(jnp.bfloat16)
    kv_ext = with_halo(kv_local, (("row", 0),), HALF)
    key_span = QBLK + 2 * HALF
    outputs = []
    lse_parts = []
    for offset in range(0, queries.shape[0], QBLK):
        visible = block_visible(seg_local, seg_ext, key_ok, offset, key_span)
        scores, query_heads, key_heads = block_scores(
            queries[offset : offset + QBLK], kv_ext[offset : offset + key_span, :hd_col], visible
        )
        value_heads = kv_ext[offset : offset + key_span, hd_col:].reshape(key_span, -1, DH)
        row_max = jnp.max(scores, 2, keepdims=True)
        exp_scores = jnp.exp(scores - row_max)
        row_sum = jnp.sum(exp_scores, 2, keepdims=True)
        softmax_b = (exp_scores / row_sum).astype(jnp.bfloat16)
        lse_parts.append((row_max + jnp.log(row_sum))[:, :, 0])
        outputs.append(
            jnp.einsum(
                "hqk,khd->qhd", softmax_b, value_heads, preferred_element_type=jnp.float32
            ).reshape(QBLK, hd_col)
        )
    attended = jnp.concatenate(outputs, 0).astype(jnp.bfloat16)
    lse_all = jnp.concatenate(lse_parts, 1)
    attn_full = gather_rows(attended)
    branch = scatter_cols(attn_full, w_out, False) + bias_o
    resid_one = hidden + branch
    normed_out, normed_one, inv_one = norm_forward(resid_one, gain_one, shift_one)
    mid_full = gather_cols(normed_out.astype(jnp.bfloat16))
    up_proj = scatter_rows(mid_full, w_up, False) + bias_up
    act_full = gather_rows(gelu_exact(up_proj).astype(jnp.bfloat16))
    down_proj = scatter_cols(act_full, w_down, False) + bias_down
    layer_out, normed_two, inv_two = norm_forward(normed_out + down_proj, gain_two, shift_two)
    kept = (
        inputs_full,
        w_qkv,
        queries,
        kv_ext,
        lse_all,
        attn_full,
        normed_one,
        inv_one,
        mid_full,
        up_proj,
        act_full,
        normed_two,
        inv_two,
    )
    return (layer_out, kept, resid_one, branch)


def layer_backward(grad_out, weights, vec_row, seg_local, seg_ext, key_ok, kept):
    w_query, w_key, w_value, w_out, w_up, w_down = weights
    (
        inputs_full,
        w_qkv,
        queries,
        kv_ext,
        lse_all,
        attn_full,
        normed_one,
        inv_one,
        mid_full,
        up_proj,
        act_full,
        normed_two,
        inv_two,
    ) = kept
    hd_col = w_query.shape[1]
    spots = vector_offsets(grad_out.shape[1], hd_col, w_up.shape[1])
    vec_parts = take_parts(vec_row, spots)
    d_resid_two, d_gain_two, d_shift_two = norm_backward(
        grad_out, normed_two, inv_two, vec_parts[6]
    )
    d_down = d_resid_two.astype(jnp.bfloat16)
    d_down_full = gather_cols(d_down)
    grad_down = matmul_at(act_full, d_down_full)
    d_act = scatter_rows(d_down_full, w_down, True)
    gelu_value, gelu_back = jax.vjp(gelu_exact, up_proj)
    d_up = gelu_back(d_act)[0].astype(jnp.bfloat16)
    d_up_full = gather_rows(d_up)
    grad_up = matmul_at(mid_full, d_up_full)
    d_mid = scatter_cols(d_up_full, w_up, True)
    d_resid_one, d_gain_one, d_shift_one = norm_backward(
        d_resid_two + d_mid, normed_one, inv_one, vec_parts[4]
    )
    d_branch = d_resid_one.astype(jnp.bfloat16)
    d_branch_full = gather_cols(d_branch)
    grad_outw = matmul_at(attn_full, d_branch_full)
    d_attended = scatter_rows(d_branch_full, w_out, True).astype(jnp.bfloat16)
    key_span = QBLK + 2 * HALF
    local_len = queries.shape[0]
    dkv_ext = jnp.zeros((kv_ext.shape[0], 2 * hd_col), jnp.float32)
    d_query_parts = []
    for offset in range(0, local_len, QBLK):
        visible = block_visible(seg_local, seg_ext, key_ok, offset, key_span)
        scores, query_heads, key_heads = block_scores(
            queries[offset : offset + QBLK], kv_ext[offset : offset + key_span, :hd_col], visible
        )
        value_heads = kv_ext[offset : offset + key_span, hd_col:].reshape(key_span, -1, DH)
        softmax_w = jnp.exp(scores - lse_all[:, offset : offset + QBLK, None])
        grad_heads = d_attended[offset : offset + QBLK].reshape(QBLK, -1, DH)
        d_weights = jnp.einsum(
            "qhd,khd->hqk", grad_heads, value_heads, preferred_element_type=jnp.float32
        )
        row_dot = jnp.sum(softmax_w * d_weights, 2, keepdims=True)
        d_scores = (softmax_w * (d_weights - row_dot)).astype(jnp.bfloat16)
        d_query_parts.append(
            jnp.einsum(
                "hqk,khd->qhd", d_scores, key_heads, preferred_element_type=jnp.float32
            ).reshape(QBLK, hd_col)
            * DH ** (-0.5)
        )
        d_key_blk = jnp.einsum(
            "hqk,qhd->khd", d_scores, query_heads, preferred_element_type=jnp.float32
        ).reshape(key_span, hd_col) * DH ** (-0.5)
        d_value_blk = jnp.einsum(
            "hqk,qhd->khd",
            softmax_w.astype(jnp.bfloat16),
            grad_heads,
            preferred_element_type=jnp.float32,
        ).reshape(key_span, hd_col)
        dkv_ext = dkv_ext.at[offset : offset + key_span].add(
            jnp.concatenate((d_key_blk, d_value_blk), 1)
        )
    rim_rows = jnp.concatenate((dkv_ext[:HALF], dkv_ext[HALF + local_len :]), 0)
    returned = with_halo(rim_rows.astype(jnp.bfloat16), (("row", 0),), HALF).astype(rim_rows.dtype)
    d_kv = dkv_ext[HALF : HALF + local_len]
    d_kv = d_kv.at[:HALF].add(returned[:HALF])
    d_kv = d_kv.at[local_len - HALF :].add(returned[3 * HALF :])
    d_qkv = jnp.concatenate((jnp.concatenate(d_query_parts, 0), d_kv), 1).astype(jnp.bfloat16)
    d_qkv_full = gather_rows(d_qkv)
    grad_qkv = matmul_at(inputs_full, d_qkv_full)
    d_inputs = scatter_cols(d_qkv_full, w_qkv, True)
    d_hidden = d_resid_one + d_inputs
    d_qkv_wide = d_qkv.astype(jnp.float32)
    pieces = (
        jnp.sum(d_qkv_wide[:, :hd_col], 0),
        jnp.sum(d_qkv_wide[:, 2 * hd_col :], 0),
        jnp.sum(d_branch.astype(jnp.float32), 0),
        jnp.sum(d_down.astype(jnp.float32), 0),
        d_gain_one,
        d_shift_one,
        d_gain_two,
        d_shift_two,
        jnp.sum(d_up.astype(jnp.float32), 0),
    )
    vec_grad_row = place_parts(pieces, spots, vec_row.shape[0])
    tile_list = jnp.concatenate(
        (
            block_tiles(grad_qkv[:, :hd_col]),
            block_tiles(grad_qkv[:, hd_col : 2 * hd_col]),
            block_tiles(grad_qkv[:, 2 * hd_col :]),
            block_tiles(grad_outw),
            block_tiles(grad_up),
            block_tiles(grad_down),
        ),
        0,
    )
    return (d_hidden, vec_grad_row, tile_list)


def rotate_update(grad_tiles, left_basis, right_basis, old_m, old_v):
    turned = jnp.einsum("...ji,...jk->...ik", left_basis, grad_tiles, precision=HIGHEST)
    rotated = jnp.einsum("...ik,...kl->...il", turned, right_basis, precision=HIGHEST)
    new_m = DECAY * old_m + (1.0 - DECAY) * rotated
    new_v = DECAY * old_v + (1.0 - DECAY) * rotated * rotated
    direction = new_m / (jnp.sqrt(new_v) + ADAM_EPS)
    back_turn = jnp.einsum("...ij,...jk->...ik", left_basis, direction, precision=HIGHEST)
    update = -TILE_RATE * jnp.einsum(
        "...ik,...lk->...il", back_turn, right_basis, precision=HIGHEST
    )
    return (new_m, new_v, update)


def body(
    tokens,
    cotangent,
    segments,
    valid,
    w_query,
    w_key,
    w_value,
    w_out,
    w_up,
    w_down,
    vectors,
    vector_m,
    vector_v,
    tile_order,
    basis_left,
    basis_right,
    tile_m,
    tile_v,
):
    seg_local = segments[0]
    local_len = seg_local.shape[0]
    seg_ext = with_halo(seg_local, (("row", 0),), HALF)
    key_pos = lax.axis_index("row") * local_len - HALF + jnp.arange(local_len + 2 * HALF)
    key_ok = (key_pos >= 0) & (key_pos < local_len * lax.axis_size("row"))
    mask_rows = valid[0].astype(jnp.float32)
    hidden = tokens[0].astype(jnp.float32)
    kept_layers = []
    for layer_pos in range(LAYERS):
        weights = (
            w_query[layer_pos],
            w_key[layer_pos],
            w_value[layer_pos],
            w_out[layer_pos],
            w_up[layer_pos],
            w_down[layer_pos],
        )
        hidden, kept, resid_one, branch = layer_forward(
            hidden, weights, vectors[layer_pos], seg_local, seg_ext, key_ok
        )
        kept_layers.append(kept)
        if layer_pos == 0:
            resid_sum = jnp.sum(mask_rows * jnp.sum(resid_one * resid_one, 1))
            branch_sum = jnp.sum(mask_rows * jnp.sum(branch * branch, 1))
            valid_count = jnp.where(lax.axis_index("row") == 0, jnp.sum(mask_rows), 0.0)
            resid_total, branch_total, count_total = lax.psum(
                (resid_sum, branch_sum, valid_count), ("dp", "row", "col")
            )
    final_out = hidden.astype(jnp.bfloat16)
    owner_code = tile_order[0, 0]
    slot_count = tile_m.shape[2]
    owners = lax.axis_size("dp")
    targets = owner_code % owners * slot_count + owner_code // owners
    grad_flow = cotangent[0].astype(jnp.float32) * mask_rows[:, None]
    vec_rows = [None] * LAYERS
    tile_lists = [None] * LAYERS
    for layer_pos in reversed(range(LAYERS)):
        weights = (
            w_query[layer_pos],
            w_key[layer_pos],
            w_value[layer_pos],
            w_out[layer_pos],
            w_up[layer_pos],
            w_down[layer_pos],
        )
        grad_flow, vec_row_grad, tile_list = layer_backward(
            grad_flow,
            weights,
            vectors[layer_pos],
            seg_local,
            seg_ext,
            key_ok,
            kept_layers[layer_pos],
        )
        vec_rows[layer_pos] = vec_row_grad
        tile_lists[layer_pos] = tile_list
    outbox = (
        jnp.zeros((owners * slot_count, TILE, TILE), jnp.float32)
        .at[targets]
        .set(jnp.concatenate(tile_lists, 0))
    )
    tile_grad = lax.psum_scatter(outbox, "dp", scatter_dimension=0, tiled=True)
    vec_local = jnp.stack(vec_rows, 0)
    vector_grad = lax.psum(vec_local, ("dp", "row", "col"))
    statistics = jnp.sqrt(jnp.stack((resid_total, branch_total)) / (D * count_total))
    vector_m_new = DECAY * vector_m + (1.0 - DECAY) * vector_grad
    vector_v_new = DECAY * vector_v + (1.0 - DECAY) * vector_grad * vector_grad
    vector_update = -VECTOR_RATE * vector_m_new / (jnp.sqrt(vector_v_new) + ADAM_EPS)
    tile_m_new, tile_v_new, tile_update = rotate_update(
        tile_grad, basis_left[0, 0], basis_right[0, 0], tile_m[0, 0], tile_v[0, 0]
    )
    return (
        final_out[None],
        grad_flow[None],
        statistics,
        vector_grad,
        vector_m_new,
        vector_v_new,
        vector_update,
        tile_grad[None, None],
        tile_m_new[None, None],
        tile_v_new[None, None],
        tile_update[None, None],
    )


def solution(mesh):
    in_specs = (
        P("dp", "col", "row"),
        P("dp", "col", "row"),
        P("dp", "row"),
        P("dp", "col"),
        P(None, "row", "col"),
        P(None, "row", "col"),
        P(None, "row", "col"),
        P(None, "col", "row"),
        P(None, "row", "col"),
        P(None, "col", "row"),
        P(),
        P(),
        P(),
        P("row", "col", None),
        P("row", "col", "dp", None, None),
        P("row", "col", "dp", None, None),
        P("row", "col", "dp", None, None),
        P("row", "col", "dp", None, None),
    )
    out_specs = (
        P("dp", "col", "row"),
        P("dp", "col", "row"),
        P(),
        P(),
        P(),
        P(),
        P(),
        P("row", "col", "dp", None, None),
        P("row", "col", "dp", None, None),
        P("row", "col", "dp", None, None),
        P("row", "col", "dp", None, None),
    )
    return jax.shard_map(body, mesh=mesh, in_specs=in_specs, out_specs=out_specs, check_vma=False)
```

profile of v0, /device:TPU:0, one launch (start us, length us, event | category | flops | bytes accessed | tf_op | source)
XLA Modules:
  0.0 1753.8 jit_solution(15898065075984570602)
XLA Ops:
  11.5 28.0 %all-gather.48.cloned.1.call-done = bf16[1,2048,384]{2,1,0:T(8,128)(2,1)} async-done(((bf16[1,1024,384]{2,1,0:T(8,128)(2,1)}), bf16[1,2048,384]{2,1,0:T(8,128)(2,1)}) %all-gather.48.cloned.1.call-update) | async-done | bytes 1572880 | tf_op jit(solution)/shard_map/all_gather | solution.py:53
  52.6 11.9 reduce-scatter.18.cloned.1.call-done
  138.5 11.8 all-gather.18.cloned.1.call-done
  154.1 27.4 %reduce-scatter.20.cloned.1.call-done = bf16[1024,384]{1,0:T(8,128)(2,1)} async-done(((bf16[2048,384]{1,0:T(8,128)(2,1)}), bf16[1024,384]{1,0:T(8,128)(2,1)}) %reduce-scatter.20.cloned.1.call-update) | async-done | bytes 786448 | tf_op jit(solution)/shard_map/reduce_scatter | solution.py:70
  188.2 27.3 %all-gather.20.cloned.1.call-done = bf16[2048,384]{1,0:T(8,128)(2,1)} async-done(((bf16[1024,384]{1,0:T(8,128)(2,1)}), bf16[2048,384]{1,0:T(8,128)(2,1)}) %all-gather.20.cloned.1.call-update) | async-done | bytes 1572880 | tf_op jit(solution)/shard_map/all_gather | solution.py:53
  215.5 9.7 fusion.98
  225.3 19.7 %reduce-scatter.22.cloned.1.call-done = f32[1024,1536]{1,0:T(8,128)} async-done(((f32[2048,1536]{1,0:T(8,128)}), f32[1024,1536]{1,0:T(8,128)}) %reduce-scatter.22.cloned.1.call-update) | async-done | bytes 6291472 | tf_op jit(solution)/shard_map/reduce_scatter | solution.py:61
  245.0 16.5 multiply_convert_fusion.5
  261.6 20.4 %all-gather.22.cloned.1.call-done = bf16[2048,1536]{1,0:T(8,128)(2,1)} async-done(((bf16[1024,1536]{1,0:T(8,128)(2,1)}), bf16[2048,1536]{1,0:T(8,128)(2,1)}) %all-gather.22.cloned.1.call-update) | async-done | bytes 6291472 | tf_op jit(solution)/shard_map/all_gather | solution.py:57
  289.7 27.4 %reduce-scatter.24.cloned.1.call-done = bf16[1024,384]{1,0:T(8,128)(2,1)} async-done(((bf16[2048,384]{1,0:T(8,128)(2,1)}), bf16[1024,384]{1,0:T(8,128)(2,1)}) %reduce-scatter.24.cloned.1.call-update) | async-done | bytes 786448 | tf_op jit(solution)/shard_map/reduce_scatter | solution.py:70
  323.4 27.3 %all-gather.24.cloned.1.call-done = bf16[2048,384]{1,0:T(8,128)(2,1)} async-done(((bf16[1024,384]{1,0:T(8,128)(2,1)}), bf16[2048,384]{1,0:T(8,128)(2,1)}) %all-gather.24.cloned.1.call-update) | async-done | bytes 1572880 | tf_op jit(solution)/shard_map/all_gather | solution.py:53
  358.9 17.3 reduce-scatter.26.cloned.1.call-done
  465.5 12.7 all-gather.26.cloned.1.call-done
  481.9 27.4 %reduce-scatter.28.cloned.1.call-done = bf16[1024,384]{1,0:T(8,128)(2,1)} async-done(((bf16[2048,384]{1,0:T(8,128)(2,1)}), bf16[1024,384]{1,0:T(8,128)(2,1)}) %reduce-scatter.28.cloned.1.call-update) | async-done | bytes 786448 | tf_op jit(solution)/shard_map/reduce_scatter | solution.py:70
  515.5 27.3 %all-gather.28.cloned.1.call-done = bf16[2048,384]{1,0:T(8,128)(2,1)} async-done(((bf16[1024,384]{1,0:T(8,128)(2,1)}), bf16[2048,384]{1,0:T(8,128)(2,1)}) %all-gather.28.cloned.1.call-update) | async-done | bytes 1572880 | tf_op jit(solution)/shard_map/all_gather | solution.py:53
  542.8 9.7 fusion.92
  552.6 20.8 %reduce-scatter.30.cloned.1.call-done = f32[1024,1536]{1,0:T(8,128)} async-done(((f32[2048,1536]{1,0:T(8,128)}), f32[1024,1536]{1,0:T(8,128)}) %reduce-scatter.30.cloned.1.call-update) | async-done | bytes 6291472 | tf_op jit(solution)/shard_map/reduce_scatter | solution.py:61
  573.5 16.3 multiply_convert_fusion.4
  589.8 19.4 %all-gather.30.cloned.1.call-done = bf16[2048,1536]{1,0:T(8,128)(2,1)} async-done(((bf16[1024,1536]{1,0:T(8,128)(2,1)}), bf16[2048,1536]{1,0:T(8,128)(2,1)}) %all-gather.30.cloned.1.call-update) | async-done | bytes 6291472 | tf_op jit(solution)/shard_map/all_gather | solution.py:57
  617.0 27.4 %reduce-scatter.32.cloned.1.call-done = bf16[1024,384]{1,0:T(8,128)(2,1)} async-done(((bf16[2048,384]{1,0:T(8,128)(2,1)}), bf16[1024,384]{1,0:T(8,128)(2,1)}) %reduce-scatter.32.cloned.1.call-update) | async-done | bytes 786448 | tf_op jit(solution)/shard_map/reduce_scatter | solution.py:70
  658.9 27.3 %all-gather.32.cloned.1.call-done = bf16[2048,384]{1,0:T(8,128)(2,1)} async-done(((bf16[1024,384]{1,0:T(8,128)(2,1)}), bf16[2048,384]{1,0:T(8,128)(2,1)}) %all-gather.32.cloned.1.call-update) | async-done | bytes 1572880 | tf_op jit(solution)/shard_map/all_gather | solution.py:53
  686.2 9.7 fusion.88
  696.0 20.8 %reduce-scatter.34.cloned.1.call-done = f32[1024,1536]{1,0:T(8,128)} async-done(((f32[2048,1536]{1,0:T(8,128)}), f32[1024,1536]{1,0:T(8,128)}) %reduce-scatter.34.cloned.1.call-update) | async-done | bytes 6291472 | tf_op jit(solution)/shard_map/reduce_scatter | solution.py:61
  716.8 10.2 convert_reduce_fusion
  727.1 19.3 %all-gather.34.cloned.1.call-done = bf16[2048,1536]{1,0:T(8,128)(2,1)} async-done(((bf16[1024,1536]{1,0:T(8,128)(2,1)}), bf16[2048,1536]{1,0:T(8,128)(2,1)}) %all-gather.34.cloned.1.call-update) | async-done | bytes 6291472 | tf_op jit(solution)/shard_map/all_gather | solution.py:57
  754.1 27.4 %reduce-scatter.36.cloned.1.call-done = bf16[1024,384]{1,0:T(8,128)(2,1)} async-done(((bf16[2048,384]{1,0:T(8,128)(2,1)}), bf16[1024,384]{1,0:T(8,128)(2,1)}) %reduce-scatter.36.cloned.1.call-update) | async-done | bytes 786448 | tf_op jit(solution)/shard_map/reduce_scatter | solution.py:70
  790.9 27.3 %all-gather.36.cloned.1.call-done = bf16[2048,384]{1,0:T(8,128)(2,1)} async-done(((bf16[1024,384]{1,0:T(8,128)(2,1)}), bf16[2048,384]{1,0:T(8,128)(2,1)}) %all-gather.36.cloned.1.call-update) | async-done | bytes 1572880 | tf_op jit(solution)/shard_map/all_gather | solution.py:53
  822.9 10.8 reduce-scatter.38.cloned.1.call-done
  845.0 12.1 multiply_reduce_fusion.3
  857.3 9.6 fusion.12
  866.9 12.2 multiply_reduce_fusion.2
  879.1 14.2 multiply_convert_fusion.3
  902.1 12.9 multiply_convert_fusion.2
  945.5 15.8 all-gather.38.cloned.1.call-done
  967.8 27.4 %reduce-scatter.40.cloned.1.call-done = bf16[1024,384]{1,0:T(8,128)(2,1)} async-done(((bf16[2048,384]{1,0:T(8,128)(2,1)}), bf16[1024,384]{1,0:T(8,128)(2,1)}) %reduce-scatter.40.cloned.1.call-update) | async-done | bytes 786448 | tf_op jit(solution)/shard_map/reduce_scatter | solution.py:70
  1004.6 27.1 %all-gather.40.cloned.1.call-done = bf16[2048,384]{1,0:T(8,128)(2,1)} async-done(((bf16[1024,384]{1,0:T(8,128)(2,1)}), bf16[2048,384]{1,0:T(8,128)(2,1)}) %all-gather.40.cloned.1.call-update) | async-done | bytes 1572880 | tf_op jit(solution)/shard_map/all_gather | solution.py:53
  1031.7 9.7 fusion.94
  1041.5 20.8 %reduce-scatter.42.cloned.1.call-done = f32[1024,1536]{1,0:T(8,128)} async-done(((f32[2048,1536]{1,0:T(8,128)}), f32[1024,1536]{1,0:T(8,128)}) %reduce-scatter.42.cloned.1.call-update) | async-done | bytes 6291472 | tf_op jit(solution)/shard_map/reduce_scatter | solution.py:61
  1072.1 19.2 %all-gather.42.cloned.1.call-done = bf16[2048,1536]{1,0:T(8,128)(2,1)} async-done(((bf16[1024,1536]{1,0:T(8,128)(2,1)}), bf16[2048,1536]{1,0:T(8,128)(2,1)}) %all-gather.42.cloned.1.call-update) | async-done | bytes 6291472 | tf_op jit(solution)/shard_map/all_gather | solution.py:57
  1099.0 27.4 %reduce-scatter.44.cloned.1.call-done = bf16[1024,384]{1,0:T(8,128)(2,1)} async-done(((bf16[2048,384]{1,0:T(8,128)(2,1)}), bf16[1024,384]{1,0:T(8,128)(2,1)}) %reduce-scatter.44.cloned.1.call-update) | async-done | bytes 786448 | tf_op jit(solution)/shard_map/reduce_scatter | solution.py:70
  1135.5 27.3 %all-gather.44.cloned.1.call-done = bf16[2048,384]{1,0:T(8,128)(2,1)} async-done(((bf16[1024,384]{1,0:T(8,128)(2,1)}), bf16[2048,384]{1,0:T(8,128)(2,1)}) %all-gather.44.cloned.1.call-update) | async-done | bytes 1572880 | tf_op jit(solution)/shard_map/all_gather | solution.py:53
  1213.0 12.1 multiply_reduce_fusion.1
  1234.9 12.2 multiply_reduce_fusion
  1247.1 14.2 multiply_convert_fusion.1
  1270.2 12.9 multiply_convert_fusion
  1407.1 40.2 %scatter_fusion = f32[216,128,128]{2,1,0:T(8,128)} fusion(f32[216,128,128]{2,1,0:T(8,128)} %broadcast_in_dim.61, s32[216]{0:T(256)S(1)} %bitcast.389, f32[216,128,128]{2,1,0:T(8,128)} %constant_dynamic-update-slice_fusion), kind=kCustom, calls=%fused_computation | custom fusion | bytes 42468192 | tf_op jit(solution)/shard_map/scatter | solution.py:426
  1449.9 40.2 %all-reduce.2 = (f32[1]{0:T(128)}, f32[1]{0:T(128)}, f32[]{:T(128)}) all-reduce(f32[1]{0:T(128)} %bitcast.71, f32[1]{0:T(128)} %bitcast.70, f32[]{:T(128)S(6)} %select_n.128), channel_id=1, replica_groups=mesh['dp'=8,'row'=2,'col'=2] {'dp','row','col'}, use_global_device_ids=true, to_apply=%region_64.65 | all-reduce | flops 3 | bytes 24 | tf_op jit(solution)/shard_map/psum | solution.py:392
  1498.2 231.1 %reduce-scatter.50.cloned.1.call-done = f32[27,128,128]{2,1,0:T(8,128)} async-done(((f32[216,128,128]{2,1,0:T(8,128)}), f32[27,128,128]{2,1,0:T(8,128)}) %reduce-scatter.50.cloned.1.call-update) | async-done | bytes 1769488 | tf_op jit(solution)/shard_map/reduce_scatter | solution.py:428
  (572 shorter events, 578.7 us)
Async XLA Ops:
  7.2 1722.1 %copy-start = (f32[1,1,27,128,128]{4,3,2,1,0:T(8,128)S(1)}, f32[1,1,27,128,128]{4,3,2,1,0:T(8,128)}, u32[]{:S(2)}) copy-start(f32[1,1,27,128,128]{4,3,2,1,0:T(8,128)} %param.48) | copy-start | bytes 5308420
  7.2 32.3 %all-gather.48.cloned.1.call-start = ((), (), s32[]{:S(2)}) async-start(), calls=%async_computation.50 | async-start | bytes 2359296 | tf_op jit(solution)/shard_map/all_gather | solution.py:53
  7.9 56.6 %reduce-scatter.18.cloned.1.call-start = ((), (), s32[]{:S(2)}) async-start(), calls=%async_computation.17 | async-start | bytes 14155776 | tf_op jit(solution)/shard_map/reduce_scatter | solution.py:61
  47.3 103.0 %all-gather.18.cloned.1.call-start = ((), (), s32[]{:S(2)}) async-start(), calls=%async_computation.18 | async-start | bytes 2359296 | tf_op jit(solution)/shard_map/all_gather | solution.py:57
  47.9 3.1 collective-permute-start.1
  49.5 3.1 collective-permute-start.3
  51.0 266.1 %copy-start.84 = (f32[384]{0:T(512)}, f32[384]{0:T(512)S(1)}, u32[]{:S(2)}) copy-start(f32[384]{0:T(512)S(1)} %get-tuple-element.149) | copy-start | bytes 4612
  51.0 266.1 %copy-start.95 = (f32[384]{0:T(512)}, f32[384]{0:T(512)S(1)}, u32[]{:S(2)}) copy-start(f32[384]{0:T(512)S(1)} %get-tuple-element.148) | copy-start | bytes 4612
  68.3 6.8 collective-permute-start
  70.6 4.6 collective-permute-start.2
  138.4 43.1 %reduce-scatter.20.cloned.1.call-start = ((), (), s32[]{:S(2)}) async-start(), calls=%async_computation.19 | async-start | bytes 2359296 | tf_op jit(solution)/shard_map/reduce_scatter | solution.py:70
  154.1 61.5 %all-gather.20.cloned.1.call-start = ((), (), s32[]{:S(2)}) async-start(), calls=%async_computation.20 | async-start | bytes 2359296 | tf_op jit(solution)/shard_map/all_gather | solution.py:53
  188.2 56.8 %reduce-scatter.22.cloned.1.call-start = ((), (), s32[]{:S(2)}) async-start(), calls=%async_computation.21 | async-start | bytes 18874368 | tf_op jit(solution)/shard_map/reduce_scatter | solution.py:61
  225.2 56.7 %all-gather.22.cloned.1.call-start = ((), (), s32[]{:S(2)}) async-start(), calls=%async_computation.22 | async-start | bytes 9437184 | tf_op jit(solution)/shard_map/all_gather | solution.py:57
  261.5 55.6 %reduce-scatter.24.cloned.1.call-start = ((), (), s32[]{:S(2)}) async-start(), calls=%async_computation.23 | async-start | bytes 2359296 | tf_op jit(solution)/shard_map/reduce_scatter | solution.py:70
  289.6 61.1 %all-gather.24.cloned.1.call-start = ((), (), s32[]{:S(2)}) async-start(), calls=%async_computation.24 | async-start | bytes 2359296 | tf_op jit(solution)/shard_map/all_gather | solution.py:53
  323.4 52.8 %reduce-scatter.26.cloned.1.call-start = ((), (), s32[]{:S(2)}) async-start(), calls=%async_computation.25 | async-start | bytes 14155776 | tf_op jit(solution)/shard_map/reduce_scatter | solution.py:61
  358.8 119.4 %all-gather.26.cloned.1.call-start = ((), (), s32[]{:S(2)}) async-start(), calls=%async_computation.26 | async-start | bytes 2359296 | tf_op jit(solution)/shard_map/all_gather | solution.py:57
  381.0 9.2 collective-permute-start.4
  384.1 6.1 collective-permute-start.5
  465.4 44.0 %reduce-scatter.28.cloned.1.call-start = ((), (), s32[]{:S(2)}) async-start(), calls=%async_computation.27 | async-start | bytes 2359296 | tf_op jit(solution)/shard_map/reduce_scatter | solution.py:70
  481.9 61.0 %all-gather.28.cloned.1.call-start = ((), (), s32[]{:S(2)}) async-start(), calls=%async_computation.28 | async-start | bytes 2359296 | tf_op jit(solution)/shard_map/all_gather | solution.py:53
  515.5 58.0 %reduce-scatter.30.cloned.1.call-start = ((), (), s32[]{:S(2)}) async-start(), calls=%async_computation.29 | async-start | bytes 18874368 | tf_op jit(solution)/shard_map/reduce_scatter | solution.py:61
  552.6 56.7 %all-gather.30.cloned.1.call-start = ((), (), s32[]{:S(2)}) async-start(), calls=%async_computation.30 | async-start | bytes 9437184 | tf_op jit(solution)/shard_map/all_gather | solution.py:57
  589.8 54.6 %reduce-scatter.32.cloned.1.call-start = ((), (), s32[]{:S(2)}) async-start(), calls=%async_computation.31 | async-start | bytes 2359296 | tf_op jit(solution)/shard_map/reduce_scatter | solution.py:70
  616.9 69.3 %all-gather.32.cloned.1.call-start = ((), (), s32[]{:S(2)}) async-start(), calls=%async_computation.32 | async-start | bytes 2359296 | tf_op jit(solution)/shard_map/all_gather | solution.py:53
  658.8 58.0 %reduce-scatter.34.cloned.1.call-start = ((), (), s32[]{:S(2)}) async-start(), calls=%async_computation.33 | async-start | bytes 18874368 | tf_op jit(solution)/shard_map/reduce_scatter | solution.py:61
  695.9 50.4 %all-gather.34.cloned.1.call-start = ((), (), s32[]{:S(2)}) async-start(), calls=%async_computation.34 | async-start | bytes 9437184 | tf_op jit(solution)/shard_map/all_gather | solution.py:57
  727.1 54.5 %reduce-scatter.36.cloned.1.call-start = ((), (), s32[]{:S(2)}) async-start(), calls=%async_computation.35 | async-start | bytes 2359296 | tf_op jit(solution)/shard_map/reduce_scatter | solution.py:70
  754.1 64.1 %all-gather.36.cloned.1.call-start = ((), (), s32[]{:S(2)}) async-start(), calls=%async_computation.36 | async-start | bytes 2359296 | tf_op jit(solution)/shard_map/all_gather | solution.py:53
  790.8 42.9 %reduce-scatter.38.cloned.1.call-start = ((), (), s32[]{:S(2)}) async-start(), calls=%async_computation.37 | async-start | bytes 4718592 | tf_op jit(solution)/shard_map/reduce_scatter | solution.py:61
  822.4 139.0 %all-gather.38.cloned.1.call-start = ((), (), s32[]{:S(2)}) async-start(), calls=%async_computation.38 | async-start | bytes 7077888 | tf_op jit(solution)/shard_map/all_gather | solution.py:57
  920.6 19.5 %collective-permute-start.7 = (bf16[512,768]{0,1:T(8,128)(2,1)S(1)}, bf16[512,768]{0,1:T(8,128)(2,1)S(1)}, u32[]{:S(2)}, u32[]{:S(2)}) collective-permute-start(bf16[512,768]{0,1:T(8,128)(2,1)S(1)} %fusion.53), channel_id=1, source_target_pairs={{2,0},{3,1},{6,4},{7,5},{10,8},{11,9},{14,12},{15,13},{18,16},{19,... | collective-permute-start | bytes 2359304 | tf_op jit(solution)/shard_map/ppermute | solution.py:31
  925.0 15.1 collective-permute-start.6
  945.5 49.7 %reduce-scatter.40.cloned.1.call-start = ((), (), s32[]{:S(2)}) async-start(), calls=%async_computation.39 | async-start | bytes 2359296 | tf_op jit(solution)/shard_map/reduce_scatter | solution.py:70
  967.7 64.0 %all-gather.40.cloned.1.call-start = ((), (), s32[]{:S(2)}) async-start(), calls=%async_computation.40 | async-start | bytes 2359296 | tf_op jit(solution)/shard_map/all_gather | solution.py:53
  1004.4 58.0 %reduce-scatter.42.cloned.1.call-start = ((), (), s32[]{:S(2)}) async-start(), calls=%async_computation.41 | async-start | bytes 18874368 | tf_op jit(solution)/shard_map/reduce_scatter | solution.py:61
  1041.5 49.8 %all-gather.42.cloned.1.call-start = ((), (), s32[]{:S(2)}) async-start(), calls=%async_computation.42 | async-start | bytes 9437184 | tf_op jit(solution)/shard_map/all_gather | solution.py:57
  1072.0 54.4 %reduce-scatter.44.cloned.1.call-start = ((), (), s32[]{:S(2)}) async-start(), calls=%async_computation.43 | async-start | bytes 2359296 | tf_op jit(solution)/shard_map/reduce_scatter | solution.py:70
  1098.9 63.9 %all-gather.44.cloned.1.call-start = ((), (), s32[]{:S(2)}) async-start(), calls=%async_computation.44 | async-start | bytes 2359296 | tf_op jit(solution)/shard_map/all_gather | solution.py:53
  1135.5 66.2 %reduce-scatter.46.cloned.1.call-start = ((), (), s32[]{:S(2)}) async-start(), calls=%async_computation.45 | async-start | bytes 4718592 | tf_op jit(solution)/shard_map/reduce_scatter | solution.py:61
  1167.1 176.8 %all-gather.46.cloned.1.call-start = ((), (), s32[]{:S(2)}) async-start(), calls=%async_computation.46 | async-start | bytes 7077888 | tf_op jit(solution)/shard_map/all_gather | solution.py:57
  1288.6 19.3 %collective-permute-start.9 = (bf16[512,768]{0,1:T(8,128)(2,1)S(1)}, bf16[512,768]{0,1:T(8,128)(2,1)S(1)}, u32[]{:S(2)}, u32[]{:S(2)}) collective-permute-start(bf16[512,768]{0,1:T(8,128)(2,1)S(1)} %fusion.51), channel_id=1, source_target_pairs={{2,0},{3,1},{6,4},{7,5},{10,8},{11,9},{14,12},{15,13},{18,16},{19,... | collective-permute-start | bytes 2359304 | tf_op jit(solution)/shard_map/ppermute | solution.py:31
  1292.9 15.1 collective-permute-start.8
  1313.4 179.2 %all-reduce.13.cloned.1.call-start = ((), (), s32[]{:S(2)}) async-start(), calls=%async_computation.48 | async-start | bytes 147456 | tf_op jit(solution)/shard_map/psum | solution.py:430
  1343.8 152.0 %reduce-scatter.48.cloned.1.call-start = ((), (), s32[]{:S(2)}) async-start(), calls=%async_computation.47 | async-start | bytes 2359296 | tf_op jit(solution)/shard_map/reduce_scatter | solution.py:70
  1350.5 378.8 %reduce-scatter.50.cloned.1.call-start = ((), (), s32[]{:S(2)}) async-start(), calls=%async_computation.49 | async-start | bytes 15925248 | tf_op jit(solution)/shard_map/reduce_scatter | solution.py:428
  1498.2 235.6 %copy-start.31 = (f32[1,1,27,128,128]{4,3,2,1,0:T(8,128)S(1)}, f32[1,1,27,128,128]{4,3,2,1,0:T(8,128)}, u32[]{:S(2)}) copy-start(f32[1,1,27,128,128]{4,3,2,1,0:T(8,128)} %param.49) | copy-start | bytes 5308420
  (125 other events, 1859.9 us)
Sparse Core Ops, SparseCore 0:
  9.6 29.8 all-gather.47
  47.4 17.0 reduce-scatter.17
  138.6 11.7 all-gather.17
  154.2 27.3 reduce-scatter.19
  188.3 27.1 all-gather.19
  225.4 19.6 reduce-scatter.21
  261.6 20.2 all-gather.21
  289.8 27.3 reduce-scatter.23
  323.5 27.1 all-gather.23
  358.9 17.2 reduce-scatter.25
  465.5 12.5 all-gather.25
  482.0 27.3 reduce-scatter.27
  515.6 27.1 all-gather.27
  552.7 20.7 reduce-scatter.29
  589.9 19.3 all-gather.29
  617.0 27.3 reduce-scatter.31
  659.0 27.1 all-gather.31
  696.1 20.7 reduce-scatter.33
  727.2 19.1 all-gather.33
  754.2 27.3 reduce-scatter.35
  790.9 27.1 all-gather.35
  822.5 11.1 reduce-scatter.37
  945.6 15.7 all-gather.37
  967.8 27.3 reduce-scatter.39
  1004.5 27.1 all-gather.39
  1041.6 20.7 reduce-scatter.41
  1072.1 19.1 all-gather.41
  1099.1 27.3 reduce-scatter.43
  1135.6 27.1 all-gather.43
  1167.2 11.1 reduce-scatter.45
  1313.5 14.4 all-gather.45
  1343.9 120.2 all-reduce.12
  1466.8 28.9 reduce-scatter.47
  1500.0 229.2 reduce-scatter.49
where the time goes:
time: 1760 us; the launch traced here: 1750 us
  waiting for transfers between devices  887 us (50%)
  matrix products  361 us (21%)
  other arithmetic  254 us (14%)
  local copies, waits for them, and re-layouts  150 us (9%)
  blocking collectives  60 us (3%)
  starting transfers between devices  23.6 us (1%)
  between operations  17.8 us (1%)
    reduce_scatter x1, waiting for transfers between devices, body(): tile_grad = lax.psum_scatter(outbox, 'dp', scatter_dimension=0, tiled=True)  231 us
    all_gather x8, waiting for transfers between devices, gather_cols(): return lax.all_gather(value, 'col', axis=0, tiled=True)  219 us
    reduce_scatter x8, waiting for transfers between devices, scatter_cols(): lax.psum_scatter((matmul_bt(full_rows, weight) if transposed else matmul(...  193 us
    reduce_scatter x8, waiting for transfers between devices, scatter_rows(): lax.psum_scatter(matmul_bt(full_rows, weight) if transposed else matmul(f...  122 us
    all_gather x8, waiting for transfers between devices, gather_rows(): return lax.all_gather(value, 'row', axis=0, tiled=True)  119 us
    dot_general x8, matrix products, matmul(): return jnp.dot(left_mat, right_mat, preferred_element_type=jnp.float32)  57.9 us
    dot_general x8, matrix products, matmul_bt(): lax.dot_general(left_mat, right_mat, (((1,), (1,)), ((), ())), preferred_...  56.1 us
    convert_element_type x4, other arithmetic, layer_backward(): d_scores = (softmax_w * (d_weights - row_dot)).astype(jnp.bfloat16)  54.3 us
  transfers between devices with their start and end apart: 44, of which 32 were waited for; matrix products, arithmetic and copies ran while one was open for 12% of the time, Pallas kernels for 0%

commit v1 on v0

v1 whole, which is shorter than its diff:
```python
import functools

import jax
import jax.numpy as jnp
from jax import lax
from jax.experimental import pallas as pl
from jax.experimental.pallas import tpu as pltpu
from jax.sharding import PartitionSpec as P

D = 768
DH = 64
LAYERS = 2
HALF = 512
TILE = 128
HF = 384
FFC = 1536
FT = 512
STEPS = FFC // FT
TOK = 512
QB = 128
KSPAN = QB + 2 * HALF
PAIRS = 6

HIGHEST = lax.Precision.HIGHEST
NEG_BIG = -1e30
NORM_EPS = 1e-06
ADAM_EPS = 1e-08
TILE_RATE = 0.03
VECTOR_RATE = 0.1
DECAY = 0.5
F32 = jnp.float32
BF16 = jnp.bfloat16
SWAP = ((0, 1), (1, 0))


def dot(a, b):
    return lax.dot_general(a, b, (((1,), (0,)), ((), ())), preferred_element_type=F32)


def dot_bt(a, b):
    return lax.dot_general(a, b, (((1,), (1,)), ((), ())), preferred_element_type=F32)


def dot_at(a, b):
    return lax.dot_general(a, b, (((0,), (0,)), ((), ())), preferred_element_type=F32)


def sds(shape, dtype):
    return jax.ShapeDtypeStruct(shape, dtype)


def whole(shape):
    return pl.BlockSpec(shape, lambda *_: (0,) * len(shape))


SMEM_SPEC = pl.BlockSpec(memory_space=pltpu.SMEM)


def cost(flops, nbytes):
    return pl.CostEstimate(flops=int(flops), bytes_accessed=int(nbytes), transcendentals=0)


def params():
    return pltpu.CompilerParams(vmem_limit_bytes=60 * 1024 * 1024)


def qkv_kernel(rc, x_ref, w00, w01, w10, w11, vec, q_ref, kv_ref):
    for rel_c, (w_near, w_far) in enumerate(((w00, w10), (w01, w11))):
        c = rc[1] ^ rel_c
        acc = dot(x_ref[0], w_near[...]) + dot(x_ref[1], w_far[...])
        q = (acc[:, :HF] + vec[c]).astype(BF16)
        q_ref[c] = (q.astype(F32) * DH ** (-0.5)).astype(BF16)
        kv_ref[c, 0] = acc[:, HF : 2 * HF].astype(BF16)
        kv_ref[c, 1] = (acc[:, 2 * HF :] + vec[2 + c]).astype(BF16)


def qkv_forward(rc, x, pieces, va):
    rows = 256
    return pl.pallas_call(
        qkv_kernel,
        grid=(TOK // rows,),
        in_specs=[SMEM_SPEC, pl.BlockSpec((2, rows, HF), lambda i: (0, i, 0))]
        + [whole((HF, 3 * HF))] * 4
        + [whole((16, 1, HF))],
        out_specs=[
            pl.BlockSpec((2, rows, HF), lambda i: (0, i, 0)),
            pl.BlockSpec((2, 2, rows, HF), lambda i: (0, 0, i, 0)),
        ],
        out_shape=[sds((2, TOK, HF), BF16), sds((2, 2, TOK, HF), BF16)],
        compiler_params=params(),
        cost_estimate=cost(2 * TOK * D * 3 * D, 7e6),
        name="qkv",
    )(rc, x, *pieces, va)


def fill_bias(bias, segk_ref, segq_ref, b):
    off = pl.multiple_of(b * QB, QB)
    seg_k = segk_ref[pl.ds(off, KSPAN), :]
    key = lax.broadcasted_iota(jnp.int32, (KSPAN, QB), 0)
    query = lax.broadcasted_iota(jnp.int32, (KSPAN, QB), 1)
    seen = (seg_k == segq_ref[b]) & (jnp.abs(key - query - HALF) < HALF)
    bias[b] = jnp.where(seen, 0.0, NEG_BIG).astype(F32)


def fill_keys(ext, left, own, right):
    ext[0:TOK] = left[0, 0]
    ext[TOK : 2 * TOK] = own[0, 0]
    ext[2 * TOK :] = right[0, 0]


def split_pair(block):
    lane = lax.broadcasted_iota(jnp.int32, block.shape, 1)
    zero = jnp.zeros_like(block)
    return jnp.concatenate(
        (jnp.where(lane < DH, block, zero), jnp.where(lane >= DH, block, zero)), 0
    )


def join_pair(turned):
    return jnp.concatenate((turned[:DH, :QB], turned[DH:, QB:]), 0)


def attn_fwd_kernel(
    segk_ref, segq_ref, q_ref, kl, ko, kr, vl, vo, vr, o_ref, lse_ref, kext, vturn, bias
):
    h = pl.program_id(0)
    b = pl.program_id(1)

    @pl.when(b == 0)
    def _():
        fill_keys(kext, kl, ko, kr)
        for place, part in enumerate((vl, vo, vr)):
            vturn[:, place * TOK : (place + 1) * TOK] = part[0, 0].T

    @pl.when(h == 0)
    def _():
        fill_bias(bias, segk_ref, segq_ref, b)

    off = pl.multiple_of(b * QB, QB)
    qz = split_pair(q_ref[0])
    scores = dot_bt(kext[pl.ds(off, KSPAN), :], qz)
    extra = bias[b]
    scores = scores + jnp.concatenate((extra, extra), 1)
    top = jnp.max(scores, 0, keepdims=True)
    weights = jnp.exp(scores - top)
    total = jnp.sum(weights, 0, keepdims=True)
    turned = dot(vturn[:, pl.ds(off, KSPAN)], weights.astype(BF16)) / total
    o_ref[0] = join_pair(turned).T.astype(BF16)
    lse_ref[0, 0] = top + jnp.log(total)


def pair_specs():
    def kv_spec(which):
        return pl.BlockSpec((1, 1, TOK, TILE), lambda h, b: (h // 3, which, 0, h % 3))

    q_spec = pl.BlockSpec((1, QB, TILE), lambda h, b: (h // 3, b, h % 3))
    lse_spec = pl.BlockSpec((1, 1, 1, 2 * QB), lambda h, b: (h, b, 0, 0))
    return q_spec, kv_spec(0), kv_spec(1), lse_spec


def attn_forward(segk, segq, q, kv, left, right):
    q_spec, k_spec, v_spec, lse_spec = pair_specs()
    return pl.pallas_call(
        attn_fwd_kernel,
        grid=(PAIRS, TOK // QB),
        in_specs=[whole(segk.shape), whole(segq.shape), q_spec] + [k_spec] * 3 + [v_spec] * 3,
        out_specs=[q_spec, lse_spec],
        out_shape=[sds((2, TOK, HF), BF16), sds((PAIRS, TOK // QB, 1, 2 * QB), F32)],
        scratch_shapes=[
            pltpu.VMEM((3 * TOK, TILE), BF16),
            pltpu.VMEM((TILE, 3 * TOK), BF16),
            pltpu.VMEM((TOK // QB, KSPAN, QB), F32),
        ],
        compiler_params=params(),
        cost_estimate=cost(15e9, 8e6),
        name="attn_fwd",
    )(segk, segq, q, left, kv, right, left, kv, right)


def attn_bwd_kernel(
    segk_ref, segq_ref, q_ref, g_ref, lse_ref, kl, ko, kr, vl, vo, vr,
    dq_ref, dl_ref, do_ref, dr_ref, kext, vext, kturn, bias, dk, dv,
):
    h = pl.program_id(0)
    b = pl.program_id(1)

    @pl.when(b == 0)
    def _():
        fill_keys(kext, kl, ko, kr)
        fill_keys(vext, vl, vo, vr)
        for place, part in enumerate((kl, ko, kr)):
            kturn[:, place * TOK : (place + 1) * TOK] = part[0, 0].T
        dk[...] = jnp.zeros_like(dk)
        dv[...] = jnp.zeros_like(dv)

    @pl.when(h == 0)
    def _():
        fill_bias(bias, segk_ref, segq_ref, b)

    off = pl.multiple_of(b * QB, QB)
    span = pl.ds(off, KSPAN)
    qz = split_pair(q_ref[0])
    gz = split_pair(g_ref[0])
    scores = dot_bt(kext[span, :], qz)
    extra = bias[b]
    weights = jnp.exp(scores + jnp.concatenate((extra, extra), 1) - lse_ref[0, 0])
    d_weights = dot_bt(vext[span, :], gz)
    row_dot = jnp.sum(weights * d_weights, 0, keepdims=True)
    d_scores = (weights * (d_weights - row_dot)).astype(BF16)
    dv[span, :] += dot(weights.astype(BF16), gz)
    dk[span, :] += dot(d_scores, qz)
    turned = dot(kturn[:, span], d_scores)
    dq_ref[0] = (join_pair(turned).T * DH ** (-0.5)).astype(BF16)

    @pl.when(b == TOK // QB - 1)
    def _():
        for which, grads in enumerate((dk, dv)):
            dl_ref[0, which] = grads[0:TOK].astype(BF16)
            do_ref[0, which] = grads[TOK : 2 * TOK]
            dr_ref[0, which] = grads[2 * TOK :].astype(BF16)


def attn_backward(segk, segq, q, g, lse, kv, left, right):
    q_spec, k_spec, v_spec, lse_spec = pair_specs()
    d_spec = pl.BlockSpec((1, 2, TOK, TILE), lambda h, b: (h // 3, 0, 0, h % 3))
    d_shape = (2, 2, TOK, HF)
    return pl.pallas_call(
        attn_bwd_kernel,
        grid=(PAIRS, TOK // QB),
        in_specs=[whole(segk.shape), whole(segq.shape), q_spec, q_spec, lse_spec]
        + [k_spec] * 3
        + [v_spec] * 3,
        out_specs=[q_spec, d_spec, d_spec, d_spec],
        out_shape=[
            sds((2, TOK, HF), BF16), sds(d_shape, BF16), sds(d_shape, F32), sds(d_shape, BF16),
        ],
        scratch_shapes=[
            pltpu.VMEM((3 * TOK, TILE), BF16),
            pltpu.VMEM((3 * TOK, TILE), BF16),
            pltpu.VMEM((TILE, 3 * TOK), BF16),
            pltpu.VMEM((TOK // QB, KSPAN, QB), F32),
            pltpu.VMEM((3 * TOK, TILE), F32),
            pltpu.VMEM((3 * TOK, TILE), F32),
        ],
        compiler_params=params(),
        cost_estimate=cost(30e9, 16e6),
        name="attn_bwd",
    )(segk, segq, q, g, lse, left, kv, right, left, kv, right)


def feature_sum(near, far):
    return jnp.sum(near, 1, keepdims=True) + jnp.sum(far, 1, keepdims=True)


def norm_pair(near, far):
    mean = feature_sum(near, far) / D
    near = near - mean
    far = far - mean
    inv = lax.rsqrt(feature_sum(near * near, far * far) / D + NORM_EPS)
    return near * inv, far * inv, inv


def norm_pair_back(grads, normed, inv, gains):
    dn = [g * gain for g, gain in zip(grads, gains)]
    first = feature_sum(*dn) / D
    second = feature_sum(*[d * n for d, n in zip(dn, normed)]) / D
    return [inv * (d - first - n * second) for d, n in zip(dn, normed)]


def out_kernel(rc, a_ref, w00, w01, w10, w11, hid_ref, valid_ref, vec,
               norm_ref, mid_ref, n_ref, inv_ref, stat_ref):
    keep = valid_ref[...]
    resid = []
    sums = []
    for rel_r, (w_near, w_far) in enumerate(((w00, w01), (w10, w11))):
        r = rc[0] ^ rel_r
        branch = dot(a_ref[rc[1]], w_near[...]) + dot(a_ref[rc[1] ^ 1], w_far[...]) + vec[4 + r]
        total = hid_ref[rel_r].astype(F32) + branch
        resid.append(total)
        sums.append((total * total, branch * branch))

    @pl.when(pl.program_id(0) == 0)
    def _():
        stat_ref[...] = jnp.zeros_like(stat_ref)

    for which in range(2):
        part = (sums[0][which] + sums[1][which]) * keep
        stat_ref[which] += jnp.sum(part, 0, keepdims=True)
    near, far, inv = norm_pair(*resid)
    for rel_r, n in enumerate((near, far)):
        r = rc[0] ^ rel_r
        out = n * vec[8 + r] + vec[10 + r]
        norm_ref[rel_r] = out
        mid_ref[rel_r] = out.astype(BF16)
        n_ref[rel_r] = n
    inv_ref[...] = inv


def out_forward(rc, attended, pieces, hidden, valid, va):
    rows = 256
    half = pl.BlockSpec((2, rows, HF), lambda i: (0, i, 0))
    col = pl.BlockSpec((rows, 1), lambda i: (i, 0))
    return pl.pallas_call(
        out_kernel,
        grid=(TOK // rows,),
        in_specs=[SMEM_SPEC, half] + [whole((HF, HF))] * 4 + [half, col, whole((16, 1, HF))],
        out_specs=[half, half, half, col, whole((2, 1, HF))],
        out_shape=[
            sds((2, TOK, HF), F32), sds((2, TOK, HF), BF16), sds((2, TOK, HF), F32),
            sds((TOK, 1), F32), sds((2, 1, HF), F32),
        ],
        compiler_params=params(),
        cost_estimate=cost(2 * TOK * D * D, 7e6),
        name="attn_out",
    )(rc, attended, *pieces, hidden, valid, va)


def gelu_parts(u):
    bell = jnp.exp(-0.5 * u * u)
    t = 1.0 / (1.0 + (0.3275911 * 0.7071067811865476) * jnp.abs(u))
    poly = t * (0.5 * 0.254829592 + t * (0.5 * -0.284496736 + t * (
        0.5 * 1.421413741 + t * (0.5 * -1.453152027 + t * (0.5 * 1.061405429)))))
    tail = poly * bell
    below = jnp.where(u >= 0, 1.0 - tail, tail)
    return u * below, below + u * bell * 0.3989422804014327


def up_spec(rel_c):
    return pl.BlockSpec((HF, FT), lambda f: (0, jnp.clip(f - STEPS * rel_c, 0, STEPS - 1)))


def down_spec(rel_c):
    return pl.BlockSpec((FT, HF), lambda f: (jnp.clip(f - STEPS * rel_c, 0, STEPS - 1), 0))


FFN_W_SPECS = [up_spec(0), up_spec(1)] * 2 + [down_spec(0), down_spec(1)] * 2


def ffn_fwd_kernel(rc, mid_ref, norm_ref, u00, u01, u10, u11, d00, d01, d10, d11, vec, vecu,
                   act_ref, slope_ref, hid_ref, low_ref, n_ref, inv_ref, acc):
    f = pl.program_id(0)

    @pl.when(f == 0)
    def _():
        acc[...] = jnp.zeros_like(acc)

    def step(rel_c, u_near, u_far, d_near, d_far):
        spot = (rc[1] ^ rel_c) * STEPS + f - STEPS * rel_c
        up = dot(mid_ref[0], u_near[...]) + dot(mid_ref[1], u_far[...]) + vecu[spot]
        act, slope = gelu_parts(up)
        act = act.astype(BF16)
        act_ref[...] = act
        slope_ref[...] = slope.astype(BF16)
        acc[0] += dot(act, d_near[...])
        acc[1] += dot(act, d_far[...])

    @pl.when(f < STEPS)
    def _():
        step(0, u00, u10, d00, d10)

    @pl.when(f >= STEPS)
    def _():
        step(1, u01, u11, d01, d11)

    @pl.when(f == 2 * STEPS - 1)
    def _():
        parts = [norm_ref[rel_r] + (acc[rel_r] + vec[6 + (rc[0] ^ rel_r)]) for rel_r in range(2)]
        near, far, inv = norm_pair(*parts)
        for rel_r, n in enumerate((near, far)):
            r = rc[0] ^ rel_r
            out = n * vec[12 + r] + vec[14 + r]
            hid_ref[rel_r] = out
            low_ref[rel_r] = out.astype(BF16)
            n_ref[rel_r] = n
        inv_ref[...] = inv


def ffn_forward(rc, mid, normed, ups, downs, va, vb):
    full = whole((2, TOK, HF))
    wide = pl.BlockSpec((TOK, FT), lambda f: (0, f))
    return pl.pallas_call(
        ffn_fwd_kernel,
        grid=(2 * STEPS,),
        in_specs=[SMEM_SPEC, full, full] + FFN_W_SPECS + [whole(va.shape), whole(vb.shape)],
        out_specs=[wide, wide, full, full, full, whole((TOK, 1))],
        out_shape=[
            sds((TOK, 2 * FFC), BF16), sds((TOK, 2 * FFC), BF16), sds((2, TOK, HF), F32),
            sds((2, TOK, HF), BF16), sds((2, TOK, HF), F32), sds((TOK, 1), F32),
        ],
        scratch_shapes=[pltpu.VMEM((2, TOK, HF), F32)],
        compiler_params=params(),
        cost_estimate=cost(4 * TOK * D * 4 * D, 24e6),
        name="ffn_fwd",
    )(rc, mid, normed, *ups, *downs, va, vb)


def put_tiles(ref, lead, first, block):
    rows, cols = block.shape
    spot = first
    for i in range(rows // TILE):
        for j in range(cols // TILE):
            ref[lead + (spot,)] = block[
                i * TILE : (i + 1) * TILE, j * TILE : (j + 1) * TILE
            ].astype(BF16)
            spot += 1


def ffn_bwd_kernel(rc, g_ref, n2_ref, inv2_ref, mid_ref, act_ref, slope_ref, n1_ref, inv1_ref,
                   u00, u01, u10, u11, d00, d01, d10, d11, vec,
                   gm_ref, gt_ref, dres_ref, dbr_ref, gv_ref, gu_ref, d_two, d_down, d_mid):
    f = pl.program_id(0)
    rs = [rc[0], rc[0] ^ 1]

    def note(which, rel_r, value):
        gv_ref[2 * which + rs[rel_r]] = jnp.sum(value, 0, keepdims=True)

    @pl.when(f == 0)
    def _():
        grads = [g_ref[0], g_ref[1]]
        normed = [n2_ref[0], n2_ref[1]]
        d_resid = norm_pair_back(grads, normed, inv2_ref[...], [vec[12 + r] for r in rs])
        for rel_r in range(2):
            note(4, rel_r, grads[rel_r] * normed[rel_r])
            note(5, rel_r, grads[rel_r])
            d_two[rel_r] = d_resid[rel_r]
            low = d_resid[rel_r].astype(BF16)
            d_down[rel_r] = low
            note(1, rel_r, low.astype(F32))
        d_mid[...] = jnp.zeros_like(d_mid)

    def step(rel_c, u_near, u_far, d_near, d_far):
        spot = (rc[1] ^ rel_c) * STEPS + f - STEPS * rel_c
        d_act = dot_bt(d_down[0], d_near[...]) + dot_bt(d_down[1], d_far[...])
        d_up = (d_act * slope_ref[...].astype(F32)).astype(BF16)
        gu_ref[spot] = jnp.sum(d_up.astype(F32), 0, keepdims=True)
        act = act_ref[...]
        for rel_r, (ref, u_piece) in enumerate(((gm_ref, u_near), (gt_ref, u_far))):
            put_tiles(ref, (0, 0), 0, dot_at(mid_ref[rel_r], d_up))
            put_tiles(ref, (0, 0), 12, dot_at(act, d_down[rel_r]))
            d_mid[rel_r] += dot_bt(d_up, u_piece[...])

    @pl.when(f < STEPS)
    def _():
        step(0, u00, u10, d00, d10)

    @pl.when(f >= STEPS)
    def _():
        step(1, u01, u11, d01, d11)

    @pl.when(f == 2 * STEPS - 1)
    def _():
        grads = [d_two[rel_r] + d_mid[rel_r] for rel_r in range(2)]
        normed = [n1_ref[0], n1_ref[1]]
        d_resid = norm_pair_back(grads, normed, inv1_ref[...], [vec[8 + r] for r in rs])
        for rel_r in range(2):
            note(2, rel_r, grads[rel_r] * normed[rel_r])
            note(3, rel_r, grads[rel_r])
            dres_ref[rel_r] = d_resid[rel_r]
            low = d_resid[rel_r].astype(BF16)
            dbr_ref[rel_r] = low
            note(0, rel_r, low.astype(F32))


def ffn_backward(rc, g, n2, inv2, mid, act, slope, n1, inv1, ups, downs, va):
    full = whole((2, TOK, HF))
    col = whole((TOK, 1))
    wide = pl.BlockSpec((TOK, FT), lambda f: (0, f))
    tiles = pl.BlockSpec((1, 1, 24, TILE, TILE), lambda f: (f // STEPS, f % STEPS, 0, 0, 0))
    tile_shape = sds((2, STEPS, 24, TILE, TILE), BF16)
    return pl.pallas_call(
        ffn_bwd_kernel,
        grid=(2 * STEPS,),
        in_specs=[SMEM_SPEC, full, full, col, full, wide, wide, full, col]
        + FFN_W_SPECS
        + [whole(va.shape)],
        out_specs=[tiles, tiles, full, full, whole((12, 1, HF)), whole((2 * STEPS, 1, FT))],
        out_shape=[
            tile_shape, tile_shape, sds((2, TOK, HF), F32), sds((2, TOK, HF), BF16),
            sds((12, 1, HF), F32), sds((2 * STEPS, 1, FT), F32),
        ],
        scratch_shapes=[
            pltpu.VMEM((2, TOK, HF), F32), pltpu.VMEM((2, TOK, HF), BF16),
            pltpu.VMEM((2, TOK, HF), F32),
        ],
        compiler_params=params(),
        cost_estimate=cost(8 * TOK * D * 4 * D, 36e6),
        name="ffn_bwd",
    )(rc, g, n2, inv2, mid, act, slope, n1, inv1, *ups, *downs, va)


def out_bwd_kernel(rc, dbr_ref, a_ref, w00, w01, w10, w11, da_ref, gm_ref, gt_ref):
    for rel_c, (w_near, w_far) in enumerate(((w00, w10), (w01, w11))):
        c = rc[1] ^ rel_c
        da_ref[c] = (dot_bt(dbr_ref[0], w_near[...]) + dot_bt(dbr_ref[1], w_far[...])).astype(BF16)
        rows = a_ref[c]
        put_tiles(gm_ref, (rel_c,), 0, dot_at(rows, dbr_ref[0]))
        put_tiles(gt_ref, (rel_c,), 0, dot_at(rows, dbr_ref[1]))


def out_backward(rc, d_branch, attended, pieces):
    full = whole((2, TOK, HF))
    tiles = (2, 9, TILE, TILE)
    return pl.pallas_call(
        out_bwd_kernel,
        grid=(1,),
        in_specs=[SMEM_SPEC, full, full] + [whole((HF, HF))] * 4,
        out_specs=[full, whole(tiles), whole(tiles)],
        out_shape=[sds((2, TOK, HF), BF16), sds(tiles, BF16), sds(tiles, BF16)],
        compiler_params=params(),
        cost_estimate=cost(4 * TOK * D * D, 6e6),
        name="out_bwd",
    )(rc, d_branch, attended, *pieces)


def qkv_bwd_kernel(rc, dq_ref, own_ref, left_ref, right_ref, dres_ref, x_ref, w00, w01, w10, w11,
                   dx_ref, gm_ref, gt_ref, gv_ref):
    d_near = dres_ref[0]
    d_far = dres_ref[1]
    for rel_c, (w_near, w_far) in enumerate(((w00, w10), (w01, w11))):
        c = rc[1] ^ rel_c
        parts = [dq_ref[c]]
        for which in range(2):
            back = left_ref[c, which].astype(F32) + right_ref[c, which].astype(F32)
            parts.append((own_ref[c, which] + back).astype(BF16))
        gv_ref[c] = jnp.sum(parts[0].astype(F32), 0, keepdims=True)
        gv_ref[2 + c] = jnp.sum(parts[2].astype(F32), 0, keepdims=True)
        for which in range(3):
            span = slice(which * HF, (which + 1) * HF)
            d_near += dot_bt(parts[which], w_near[:, span])
            d_far += dot_bt(parts[which], w_far[:, span])
            put_tiles(gm_ref, (rel_c,), 9 * which, dot_at(x_ref[0], parts[which]))
            put_tiles(gt_ref, (rel_c,), 9 * which, dot_at(x_ref[1], parts[which]))
    dx_ref[0] = d_near
    dx_ref[1] = d_far


def qkv_backward(rc, dq, own, left, right, d_resid, x, pieces):
    full = whole((2, TOK, HF))
    wide = whole((2, 2, TOK, HF))
    tiles = (2, 27, TILE, TILE)
    return pl.pallas_call(
        qkv_bwd_kernel,
        grid=(1,),
        in_specs=[SMEM_SPEC, full, wide, wide, wide, full, full] + [whole((HF, 3 * HF))] * 4,
        out_specs=[full, whole(tiles), whole(tiles), whole((4, 1, HF))],
        out_shape=[sds((2, TOK, HF), F32), sds(tiles, BF16), sds(tiles, BF16), sds((4, 1, HF), F32)],
        compiler_params=params(),
        cost_estimate=cost(12 * TOK * D * D, 20e6),
        name="qkv_bwd",
    )(rc, dq, own, left, right, d_resid, x, *pieces)


def row_swap(value):
    return lax.ppermute(value, "row", SWAP)


def col_swap(value):
    return lax.ppermute(value, "col", SWAP)


def four_pieces(local):
    other = col_swap(local)
    return local, other, row_swap(local), row_swap(other)


LINE_UP = ((0, 2), (2, 1), (1, 3))
LINE_DOWN = ((2, 0), (1, 2), (3, 1))


def send_up(value):
    return lax.ppermute(value, ("row", "col"), LINE_UP)


def send_down(value):
    return lax.ppermute(value, ("row", "col"), LINE_DOWN)


def add_low(*values):
    total = values[0].astype(F32)
    for value in values[1:]:
        total = total + value.astype(F32)
    return total.astype(BF16)


def pick(pair, bit):
    return lax.dynamic_index_in_dim(pair, bit, 0, keepdims=False)


def join_by(bit, near, far):
    return jnp.where(
        bit == 0, jnp.concatenate((near, far), 0), jnp.concatenate((far, near), 0)
    )


def reduce_tiles(mine, theirs):
    got = row_swap(theirs)
    away = col_swap(add_low(mine[1], got[1]))
    value = add_low(mine[0], got[0], away)
    count = value.size // (TILE * TILE)
    value = value.reshape(count * TILE, TILE)
    size = lax.axis_size("dp")
    me = lax.axis_index("dp")
    steps = []
    step = 1
    while step < size:
        steps.append(step)
        step *= 2
    for step in steps:
        bit = (me // step) % 2
        pair = value.reshape(2, value.shape[0] // 2, TILE)
        swap = [(i, i ^ step) for i in range(size)]
        value = add_low(pick(pair, bit), lax.ppermute(pick(pair, 1 - bit), "dp", swap))
    for step in reversed(steps):
        bit = (me // step) % 2
        swap = [(i, i ^ step) for i in range(size)]
        value = join_by(bit, value, lax.ppermute(value, "dp", swap))
    return value.reshape(count, TILE, TILE)


def reduce_small(value):
    value = value + row_swap(value)
    value = value + col_swap(value)
    size = lax.axis_size("dp")
    step = 1
    while step < size:
        value = value + lax.ppermute(value, "dp", [(i, i ^ step) for i in range(size)])
        step *= 2
    return value


def tile_places():
    places = []
    for layer in range(LAYERS):
        base = 108 * layer
        places += [base + i for i in range(36)]
        for rt in range(3):
            for ct in range(12):
                places.append(base + 36 + (ct // 4) * 24 + rt * 4 + ct % 4)
        for rt in range(12):
            for ct in range(3):
                places.append(base + 36 + (rt // 4) * 24 + 12 + (rt % 4) * 3 + ct)
    return places


def rotate_update(grad_tiles, left_basis, right_basis, old_m, old_v):
    turned = jnp.einsum("...ji,...jk->...ik", left_basis, grad_tiles, precision=HIGHEST)
    rotated = jnp.einsum("...ik,...kl->...il", turned, right_basis, precision=HIGHEST)
    new_m = DECAY * old_m + (1.0 - DECAY) * rotated
    new_v = DECAY * old_v + (1.0 - DECAY) * rotated * rotated
    direction = new_m / (jnp.sqrt(new_v) + ADAM_EPS)
    back_turn = jnp.einsum("...ij,...jk->...ik", left_basis, direction, precision=HIGHEST)
    update = -TILE_RATE * jnp.einsum(
        "...ik,...lk->...il", back_turn, right_basis, precision=HIGHEST
    )
    return (new_m, new_v, update)


def body(
    tokens, cotangent, segments, valid, w_query, w_key, w_value, w_out, w_up, w_down,
    vectors, vector_m, vector_v, tile_order, basis_left, basis_right, tile_m, tile_v,
):
    r = lax.axis_index("row")
    c = lax.axis_index("col")
    rc = jnp.stack((r, c)).astype(jnp.int32)

    def to_tokens(block):
        pair = block[0].reshape(2, TOK, HF)
        return jnp.stack((pick(pair, r), row_swap(pick(pair, 1 - r))), 0)

    def to_block(pair):
        return join_by(r, pair[0], row_swap(pair[1]))[None]

    x = to_tokens(tokens)
    qkv_w = [
        four_pieces(jnp.concatenate((w_query[layer], w_key[layer], w_value[layer]), 1))
        for layer in range(LAYERS)
    ]
    out_w = [four_pieces(w_out[layer]) for layer in range(LAYERS)]
    up_w = [four_pieces(w_up[layer]) for layer in range(LAYERS)]
    down_w = [four_pieces(w_down[layer]) for layer in range(LAYERS)]

    seg_full = join_by(r, segments[0], row_swap(segments[0]))
    edge = jnp.full((TOK,), -1, jnp.int32)
    seg_ext = lax.dynamic_slice_in_dim(
        jnp.concatenate((edge, seg_full, edge)), (2 * c + r) * TOK, 3 * TOK, 0
    )
    segq = seg_ext[TOK : 2 * TOK].reshape(TOK // QB, 1, QB)
    segk = seg_ext.reshape(3 * TOK, 1)
    keep = lax.dynamic_slice_in_dim(valid[0], r * TOK, TOK, 0).astype(F32).reshape(TOK, 1)
    vas = [vectors[layer, : 8 * D].reshape(16, 1, HF) for layer in range(LAYERS)]
    vbs = [vectors[layer, 8 * D :].reshape(2 * STEPS, 1, FT) for layer in range(LAYERS)]

    hidden = x
    kept = []
    stats = None
    for layer in range(LAYERS):
        q, kv = qkv_forward(rc, x, qkv_w[layer], vas[layer])
        left = send_up(kv)
        right = send_down(kv)
        attended, lse = attn_forward(segk, segq, q, kv, left, right)
        normed, mid, n1, inv1, stat = out_forward(
            rc, attended, out_w[layer], hidden, keep, vas[layer]
        )
        if layer == 0:
            stats = stat
        act, slope, hidden, x_next, n2, inv2 = ffn_forward(
            rc, mid, normed, up_w[layer], down_w[layer], vas[layer], vbs[layer]
        )
        kept.append((x, q, kv, left, right, attended, lse, mid, n1, inv1, act, slope, n2, inv2))
        x = x_next
    final_out = to_block(x)

    grad = to_tokens(cotangent).astype(F32) * keep[None]
    vec_grads = [None] * LAYERS
    tiles = [None] * LAYERS
    for layer in reversed(range(LAYERS)):
        x, q, kv, left, right, attended, lse, mid, n1, inv1, act, slope, n2, inv2 = kept[layer]
        ffn_m, ffn_t, d_resid, d_branch, gv_mid, gv_up = ffn_backward(
            rc, grad, n2, inv2, mid, act, slope, n1, inv1, up_w[layer], down_w[layer], vas[layer]
        )
        d_att, out_m, out_t = out_backward(rc, d_branch, attended, out_w[layer])
        dq, d_left, d_own, d_right = attn_backward(segk, segq, q, d_att, lse, kv, left, right)
        from_left = send_up(d_right)
        from_right = send_down(d_left)
        grad, qkv_m, qkv_t, gv_qkv = qkv_backward(
            rc, dq, d_own, from_left, from_right, d_resid, x, qkv_w[layer]
        )
        tiles[layer] = (
            reduce_tiles(qkv_m, qkv_t),
            reduce_tiles(out_m, out_t),
            reduce_tiles(
                ffn_m.reshape(2, 72, TILE, TILE), ffn_t.reshape(2, 72, TILE, TILE)
            ),
        )
        vec_grads[layer] = jnp.concatenate(
            (gv_qkv.reshape(-1), gv_mid.reshape(-1), gv_up.reshape(-1))
        )
    grad_tokens = to_block(grad)

    vec_len = vectors.shape[1]
    count = jnp.sum(keep) * 1.0
    extra = jnp.stack((jnp.sum(stats[0]), jnp.sum(stats[1]), count))
    late = reduce_small(vec_grads[0])
    early = reduce_small(jnp.concatenate((vec_grads[1], extra, jnp.zeros((125,), F32))))
    vector_grad = jnp.stack((late, early[:vec_len]), 0)
    totals = early[vec_len : vec_len + 3]
    statistics = jnp.sqrt(totals[:2] / (D * totals[2]))

    owner_code = tile_order[0, 0]
    slots = tile_m.shape[2]
    owners = lax.axis_size("dp")
    targets = owner_code % owners * slots + owner_code // owners
    my_slots = lax.axis_index("dp") * slots + jnp.arange(slots)
    match = targets[None, :] == my_slots[:, None]
    places = jnp.asarray(tile_places(), jnp.int32)
    spot = jnp.sum(jnp.where(match, places[None, :], 0), 1)
    taken = jnp.any(match, 1)
    all_tiles = jnp.concatenate(tiles[0] + tiles[1], 0)
    tile_grad = jnp.where(
        taken[:, None, None], jnp.take(all_tiles, spot, axis=0).astype(F32), 0.0
    )

    vector_m_new = DECAY * vector_m + (1.0 - DECAY) * vector_grad
    vector_v_new = DECAY * vector_v + (1.0 - DECAY) * vector_grad * vector_grad
    vector_update = -VECTOR_RATE * vector_m_new / (jnp.sqrt(vector_v_new) + ADAM_EPS)
    tile_m_new, tile_v_new, tile_update = rotate_update(
        tile_grad, basis_left[0, 0], basis_right[0, 0], tile_m[0, 0], tile_v[0, 0]
    )
    return (
        final_out,
        grad_tokens,
        statistics,
        vector_grad,
        vector_m_new,
        vector_v_new,
        vector_update,
        tile_grad[None, None],
        tile_m_new[None, None],
        tile_v_new[None, None],
        tile_update[None, None],
    )


def solution(mesh):
    weight_rc = P(None, "row", "col")
    weight_cr = P(None, "col", "row")
    slot = P("row", "col", "dp", None, None)
    block = P("dp", "col", "row")
    in_specs = (
        block, block, P("dp", "row"), P("dp", "col"),
        weight_rc, weight_rc, weight_rc, weight_cr, weight_rc, weight_cr,
        P(), P(), P(), P("row", "col", None), slot, slot, slot, slot,
    )
    out_specs = (block, block, P(), P(), P(), P(), P(), slot, slot, slot, slot)
    return jax.shard_map(body, mesh=mesh, in_specs=in_specs, out_specs=out_specs, check_vma=False)
```

time: 1760 us -> 916 us (0.52)
  waiting for transfers between devices: 887 us -> 422 us
  matrix products: 361 us -> 12.6 us
  Pallas kernels: 0 us -> 270 us
  other arithmetic: 254 us -> 65.3 us
  local copies, waits for them, and re-layouts: 150 us -> 46.6 us
  starting transfers between devices: 23.6 us -> 92.8 us
  blocking collectives: 60 us -> 0 us
    reduce_scatter x17 -> x0, waiting for transfers between devices: 547 us -> none  [the longest x1 231 us: body(): tile_grad = lax.psum_scatter(outbox, 'dp', scatter_dimension=0, tiled=True)]
    ppermute x10 -> x95, waiting for transfers between devices: 1.55 us -> 422 us  [the longest x16 257 us: col_swap(): return lax.ppermute(value, 'col', SWAP)]
    dot_general x48 -> x0, matrix products: 347 us -> none  [the longest x8 57.9 us: matmul(): return jnp.dot(left_mat, right_mat, preferred_element_type=jnp.float32)]
    all_gather x16 -> x0, waiting for transfers between devices: 337 us -> none  [the longest x8 219 us: gather_cols(): return lax.all_gather(value, 'col', axis=0, tiled=True)]
    pallas_call x0 -> x16, Pallas kernels: none -> 270 us  [the longest x2 72.5 us: attn_backward(): pl.pallas_call(attn_bwd_kernel, grid=(PAIRS, TOK // QB), in_specs=[whole(...]
    reduce_sum x22 -> x3, other arithmetic: 97.4 us -> 2.15 us  [the longest x1 1.29 us: body(): count = jnp.sum(keep) * 1.0]
    convert_element_type x16 -> x30, other arithmetic: 107 us -> 22.9 us  [add_low(): return total.astype(BF16)]
    ppermute x10 -> x95, starting transfers between devices: 20.5 us -> 92.8 us  [the longest x16 24.1 us: col_swap(): return lax.ppermute(value, 'col', SWAP)]
  transfers between devices with their start and end apart: 44 -> 95, of which waited for: 32 -> 37; matrix products, arithmetic and copies ran while one was open for 12% -> 9% of each run, Pallas kernels for 0% -> 24%
where the time goes in v1:
time: 916 us; the launch traced here: 911 us
  waiting for transfers between devices  422 us (46%)
  Pallas kernels  270 us (29%)
  starting transfers between devices  92.8 us (10%)
  other arithmetic  65.3 us (7%)
  local copies, waits for them, and re-layouts  46.6 us (5%)
  matrix products  12.6 us (1%)
    ppermute x16, waiting for transfers between devices, col_swap(): return lax.ppermute(value, 'col', SWAP)  257 us
    ppermute x18, waiting for transfers between devices, reduce_tiles(): lax.ppermute(pick(pair, 1 - bit), 'dp', swap)  86 us
    pallas_call x2, Pallas kernels, attn_backward(): pl.pallas_call(attn_bwd_kernel, grid=(PAIRS, TOK // QB), in_specs=[whole(...  72.5 us
    ppermute x18, waiting for transfers between devices, reduce_tiles(): value = join_by(bit, value, lax.ppermute(value, 'dp', swap))  62.6 us
    pallas_call x2, Pallas kernels, attn_forward(): pl.pallas_call(attn_fwd_kernel, grid=(PAIRS, TOK // QB), in_specs=[whole(...  57.8 us
    pallas_call x2, Pallas kernels, ffn_backward(): pl.pallas_call(ffn_bwd_kernel, grid=(2 * STEPS,), in_specs=[SMEM_SPEC, fu...  46.7 us
    pallas_call x2, Pallas kernels, ffn_forward(): pl.pallas_call(ffn_fwd_kernel, grid=(2 * STEPS,), in_specs=[SMEM_SPEC, fu...  36.3 us
    select_n x21, other arithmetic, join_by(): jnp.where(bit == 0, jnp.concatenate((near, far), 0), jnp.concatenate((far...  25.2 us
  transfers between devices with their start and end apart: 95, of which 37 were waited for; matrix products, arithmetic and copies ran while one was open for 9% of the time, Pallas kernels for 24%

profile of v1, /device:TPU:0, one launch (start us, length us, event | category | flops | bytes accessed | tf_op | source)
XLA Modules:
  0.0 911.2 jit_solution(16591609728726142943)
XLA Ops:
  14.9 13.1 %collective-permute-done.2.w01 = bf16[384,1152]{1,0:T(8,128)(2,1)} collective-permute-done((bf16[384,1152]{1,0:T(8,128)(2,1)}, bf16[384,1152]{1,0:T(8,128)(2,1)}, u32[]{:S(2)}, u32[]{:S(2)}) %collective-permute-start.2) | collective-permute-done | bytes 884768 | tf_op jit(solution)/shard_map/ppermute | solution.py:558
  35.8 6.2 qkv.2
  61.6 45.6 %collective-permute-done.10.u01 = bf16[384,1536]{1,0:T(8,128)(2,1)S(1)} collective-permute-done((bf16[384,1536]{1,0:T(8,128)(2,1)}, bf16[384,1536]{1,0:T(8,128)(2,1)S(1)}, u32[]{:S(2)}, u32[]{:S(2)}) %collective-permute-start.10) | collective-permute-done | bytes 1179680 | tf_op jit(solution)/shard_map/ppermute | solution.py:558
  107.7 12.2 %collective-permute-done.13.d01 = bf16[1536,384]{1,0:T(8,128)(2,1)} collective-permute-done((bf16[1536,384]{1,0:T(8,128)(2,1)}, bf16[1536,384]{1,0:T(8,128)(2,1)}, u32[]{:S(2)}, u32[]{:S(2)}) %collective-permute-start.13) | collective-permute-done | bytes 1179680 | tf_op jit(solution)/shard_map/ppermute | solution.py:558
  120.5 28.9 %attn_fwd.2 = (bf16[2,512,384]{2,1,0:T(8,128)(2,1)}, f32[6,4,1,256]{3,2,1,0:T(1,128)}) custom-call(s32[1536,1]{1,0:T(8,128)} %reshape.485.segk_ref, s32[4,1,128]{2,1,0:T(1,128)} %bitcast.335, bf16[2,512,384]{2,1,0:T(8,128)(2,1)} %get-tuple-element.73.q_ref, bf16[2,2,512,384]{3,2,1,0:T(8,128)(2,1)} %collective-permute-done.5.kl.vl, ...), custom_call_target="tpu_custom_call" | custom-call | flops 15000000512 | bytes 8000000 | tf_op jit(solution)/shard_map/attn_fwd/pallas_call | solution.py:163
  149.4 5.3 attn_out.2
  154.7 18.1 %ffn_fwd.2 = (bf16[512,3072]{1,0:T(8,128)(2,1)}, bf16[512,3072]{1,0:T(8,128)(2,1)}, f32[2,512,384]{2,1,0:T(8,128)}, bf16[2,512,384]{2,1,0:T(8,128)(2,1)}, f32[2,512,384]{2,1,0:T(8,128)}, /*index=5*/f32[512,1]{1,0:T(8,128)}) custom-call(s32[2]{0:T(128)} %pad_add_fusion.rc, bf16[2,512,384]{2,1,0:T(8,128)(2,1)} %get-tuple-element.76.mid_ref, ...), custom_call_target="tpu_custom_call" | custom-call | flops 4831838208 | bytes 24000000 | tf_op jit(solution)/shard_map/ffn_fwd/pallas_call | solution.py:381
  172.9 6.2 qkv.3
  179.1 3.5 collective-permute-start.19
  190.0 71.6 %collective-permute-done.21.w01 = bf16[384,384]{1,0:T(8,128)(2,1)S(1)} collective-permute-done((bf16[384,384]{1,0:T(8,128)(2,1)S(1)}, bf16[384,384]{1,0:T(8,128)(2,1)S(1)}, u32[]{:S(2)}, u32[]{:S(2)}) %collective-permute-start.21) | collective-permute-done | bytes 294944 | tf_op jit(solution)/shard_map/ppermute | solution.py:558
  267.0 28.9 %attn_fwd.3 = (bf16[2,512,384]{2,1,0:T(8,128)(2,1)}, f32[6,4,1,256]{3,2,1,0:T(1,128)}) custom-call(s32[1536,1]{1,0:T(8,128)} %reshape.485.segk_ref, s32[4,1,128]{2,1,0:T(1,128)} %bitcast.336, bf16[2,512,384]{2,1,0:T(8,128)(2,1)} %get-tuple-element.79.q_ref, bf16[2,2,512,384]{3,2,1,0:T(8,128)(2,1)} %collective-permute-done.19.kl.vl, ...), custom_call_target="tpu_custom_call" | custom-call | flops 15000000512 | bytes 8000000 | tf_op jit(solution)/shard_map/attn_fwd/pallas_call | solution.py:163
  296.6 5.4 attn_out.3
  302.0 18.1 %ffn_fwd.3 = (bf16[512,3072]{1,0:T(8,128)(2,1)}, bf16[512,3072]{1,0:T(8,128)(2,1)}, f32[2,512,384]{2,1,0:T(8,128)}, bf16[2,512,384]{2,1,0:T(8,128)(2,1)}, f32[2,512,384]{2,1,0:T(8,128)}, /*index=5*/f32[512,1]{1,0:T(8,128)}) custom-call(s32[2]{0:T(128)} %pad_add_fusion.rc, bf16[2,512,384]{2,1,0:T(8,128)(2,1)} %get-tuple-element.83.mid_ref, ...), custom_call_target="tpu_custom_call" | custom-call | flops 4831838208 | bytes 24000000 | tf_op jit(solution)/shard_map/ffn_fwd/pallas_call | solution.py:381
  320.2 23.2 %ffn_bwd.2 = (bf16[2,3,24,128,128]{4,3,2,1,0:T(8,128)(2,1)}, bf16[2,3,24,128,128]{4,3,2,1,0:T(8,128)(2,1)}, f32[2,512,384]{2,1,0:T(8,128)}, bf16[2,512,384]{2,1,...) custom-call(s32[2]{0:T(128)} %pad_add_fusion.rc, f32[2,512,384]{2,1,0:T(8,128)} %convert_multiply_fusion.g_ref, ...), custom_call_target="tpu_custom_call" | custom-call | flops 9663676416 | bytes 36000000 | tf_op jit(solution)/shard_map/ffn_bwd/pallas_call | solution.py:470
  343.4 4.5 out_bwd.2
  348.1 36.3 %attn_bwd.2 = (bf16[2,512,384]{2,1,0:T(8,128)(2,1)}, bf16[2,2,512,384]{3,2,1,0:T(8,128)(2,1)}, f32[2,2,512,384]{3,2,1,0:T(8,128)}, bf16[2,2,512,384]{3,2,1,0:T(8,128)(2,1)}) custom-call(s32[1536,1]{1,0:T(8,128)} %reshape.485.segk_ref, s32[4,1,128]{2,1,0:T(1,128)} %bitcast.337, bf16[2,512,384]{2,1,0:T(8,128)(2,1)} %get-tuple-element.79.q_ref, ...), custom_call_target="tpu_custom_call" | custom-call | flops 30000001024 | bytes 16000000 | tf_op jit(solution)/shard_map/attn_bwd/pallas_call | solution.py:227
  384.4 3.5 collective-permute-start.32
  393.5 21.7 %collective-permute-done.80 = bf16[9,128,128]{2,1,0:T(8,128)(2,1)S(1)} collective-permute-done((bf16[9,128,128]{2,1,0:T(8,128)(2,1)S(1)}, bf16[9,128,128]{2,1,0:T(8,128)(2,1)S(1)}, u32[]{:S(2)}, u32[]{:S(2)}) %collective-permute-start.80) | collective-permute-done | bytes 294944 | tf_op jit(solution)/shard_map/ppermute | solution.py:558
  423.8 12.1 %qkv_bwd.2 = (f32[2,512,384]{2,1,0:T(8,128)}, bf16[2,27,128,128]{3,2,1,0:T(8,128)(2,1)}, bf16[2,27,128,128]{3,2,1,0:T(8,128)(2,1)}, f32[4,1,384]{2,1,0:T(1,128)}) custom-call(s32[2]{0:T(128)} %pad_add_fusion.rc, bf16[2,512,384]{2,1,0:T(8,128)(2,1)} %get-tuple-element.95.dq_ref, f32[2,2,512,384]{3,2,1,0:T(8,128)} %get-tuple-element.96.own_ref, ...), custom_call_target="tpu_custom_call" | custom-call | flops 3623878656 | bytes 20000000 | tf_op jit(solution)/shard_map/qkv_bwd/pallas_call | solution.py:541
  436.0 23.4 %ffn_bwd.3 = (bf16[2,3,24,128,128]{4,3,2,1,0:T(8,128)(2,1)}, bf16[2,3,24,128,128]{4,3,2,1,0:T(8,128)(2,1)}, f32[2,512,384]{2,1,0:T(8,128)}, bf16[2,512,384]{2,1,...) custom-call(s32[2]{0:T(128)} %pad_add_fusion.rc, f32[2,512,384]{2,1,0:T(8,128)} %get-tuple-element.100.g_ref, ...), custom_call_target="tpu_custom_call" | custom-call | flops 9663676416 | bytes 36000000 | tf_op jit(solution)/shard_map/ffn_bwd/pallas_call | solution.py:470
  459.4 4.5 out_bwd.3
  463.9 6.4 fusion.73
  488.5 36.2 %attn_bwd.3 = (bf16[2,512,384]{2,1,0:T(8,128)(2,1)}, bf16[2,2,512,384]{3,2,1,0:T(8,128)(2,1)}, f32[2,2,512,384]{3,2,1,0:T(8,128)}, bf16[2,2,512,384]{3,2,1,0:T(8,128)(2,1)}) custom-call(s32[1536,1]{1,0:T(8,128)} %reshape.485.segk_ref, s32[4,1,128]{2,1,0:T(1,128)} %bitcast.338, bf16[2,512,384]{2,1,0:T(8,128)(2,1)} %get-tuple-element.73.q_ref, ...), custom_call_target="tpu_custom_call" | custom-call | flops 30000001024 | bytes 16000000 | tf_op jit(solution)/shard_map/attn_bwd/pallas_call | solution.py:227
  529.8 3.4 collective-permute-done.39
  534.9 4.6 collective-permute-done.86
  544.9 4.2 collective-permute-done.41
  549.7 6.5 fusion.74
  561.2 12.3 %qkv_bwd.3 = (f32[2,512,384]{2,1,0:T(8,128)}, bf16[2,27,128,128]{3,2,1,0:T(8,128)(2,1)}, bf16[2,27,128,128]{3,2,1,0:T(8,128)(2,1)}, f32[4,1,384]{2,1,0:T(1,128)}) custom-call(s32[2]{0:T(128)} %pad_add_fusion.rc, bf16[2,512,384]{2,1,0:T(8,128)(2,1)} %get-tuple-element.110.dq_ref, f32[2,2,512,384]{3,2,1,0:T(8,128)} %get-tuple-element.111.own_ref, ...), custom_call_target="tpu_custom_call" | custom-call | flops 3623878656 | bytes 20000000 | tf_op jit(solution)/shard_map/qkv_bwd/pallas_call | solution.py:541
  581.6 18.3 %collective-permute-done.43 = f32[9216]{0:T(1024)S(1)} collective-permute-done((f32[9216]{0:T(1024)S(1)}, f32[9216]{0:T(1024)S(1)}, u32[]{:S(2)}, u32[]{:S(2)}) %collective-permute-start.43) | collective-permute-done | bytes 36896 | tf_op jit(solution)/shard_map/ppermute | solution.py:558
  609.1 4.1 collective-permute-done.46
  613.2 6.2 collective-permute-done.73
  634.7 5.0 collective-permute-done.76
  640.1 54.9 %collective-permute-done.48 = bf16[27,128,128]{2,1,0:T(8,128)(2,1)S(1)} collective-permute-done((bf16[27,128,128]{2,1,0:T(8,128)(2,1)S(1)}, bf16[27,128,128]{2,1,0:T(8,128)(2,1)S(1)}, u32[]{:S(2)}, u32[]{:S(2)}) %collective-permute-start.48) | collective-permute-done | bytes 884768 | tf_op jit(solution)/shard_map/ppermute | solution.py:558
  708.9 5.9 collective-permute-done.50
  715.4 17.5 %collective-permute-done.89 = bf16[4608,128]{1,0:T(8,128)(2,1)S(1)} collective-permute-done((bf16[4608,128]{1,0:T(8,128)(2,1)S(1)}, bf16[4608,128]{1,0:T(8,128)(2,1)S(1)}, u32[]{:S(2)}, u32[]{:S(2)}) %collective-permute-start.89) | collective-permute-done | bytes 1179680 | tf_op jit(solution)/shard_map/ppermute | solution.py:612
  734.3 15.8 %collective-permute-done.64 = bf16[72,128,128]{2,1,0:T(8,128)(2,1)S(1)} collective-permute-done((bf16[72,128,128]{2,1,0:T(8,128)(2,1)S(1)}, bf16[72,128,128]{2,1,0:T(8,128)(2,1)S(1)}, u32[]{:S(2)}, u32[]{:S(2)}) %collective-permute-start.64) | collective-permute-done | bytes 2359328 | tf_op jit(solution)/shard_map/ppermute | solution.py:558
  758.2 20.0 %collective-permute-done.65 = bf16[4608,128]{1,0:T(8,128)(2,1)S(1)} collective-permute-done((bf16[4608,128]{1,0:T(8,128)(2,1)S(1)}, bf16[4608,128]{1,0:T(8,128)(2,1)S(1)}, u32[]{:S(2)}, u32[]{:S(2)}) %collective-permute-start.65) | collective-permute-done | bytes 1179680 | tf_op jit(solution)/shard_map/ppermute | solution.py:612
  781.6 18.7 %collective-permute-done.66 = bf16[2304,128]{1,0:T(8,128)(2,1)S(1)} collective-permute-done((bf16[2304,128]{1,0:T(8,128)(2,1)S(1)}, bf16[2304,128]{1,0:T(8,128)(2,1)S(1)}, u32[]{:S(2)}, u32[]{:S(2)}) %collective-permute-start.66) | collective-permute-done | bytes 589856 | tf_op jit(solution)/shard_map/ppermute | solution.py:612
  800.6 3.9 collective-permute-done.92
  808.7 4.3 collective-permute-done.67
  814.3 12.2 %collective-permute-done.93 = bf16[2304,128]{1,0:T(8,128)(2,1)S(1)} collective-permute-done((bf16[2304,128]{1,0:T(8,128)(2,1)S(1)}, bf16[2304,128]{1,0:T(8,128)(2,1)S(1)}, u32[]{:S(2)}, u32[]{:S(2)}) %collective-permute-start.93) | collective-permute-done | bytes 589856 | tf_op jit(solution)/shard_map/ppermute | solution.py:616
  829.8 10.4 %collective-permute-done.69 = bf16[2304,128]{1,0:T(8,128)(2,1)S(1)} collective-permute-done((bf16[2304,128]{1,0:T(8,128)(2,1)S(1)}, bf16[2304,128]{1,0:T(8,128)(2,1)S(1)}, u32[]{:S(2)}, u32[]{:S(2)}) %collective-permute-start.69) | collective-permute-done | bytes 589856 | tf_op jit(solution)/shard_map/ppermute | solution.py:616
  842.0 13.7 %collective-permute-done.94 = bf16[4608,128]{1,0:T(8,128)(2,1)S(1)} collective-permute-done((bf16[4608,128]{1,0:T(8,128)(2,1)S(1)}, bf16[4608,128]{1,0:T(8,128)(2,1)S(1)}, u32[]{:S(2)}, u32[]{:S(2)}) %collective-permute-start.94) | collective-permute-done | bytes 1179680 | tf_op jit(solution)/shard_map/ppermute | solution.py:616
  855.7 8.6 maximum_select_fusion.1
  864.3 12.4 %collective-permute-done.70 = bf16[4608,128]{1,0:T(8,128)(2,1)S(1)} collective-permute-done((bf16[4608,128]{1,0:T(8,128)(2,1)S(1)}, bf16[4608,128]{1,0:T(8,128)(2,1)S(1)}, u32[]{:S(2)}, u32[]{:S(2)}) %collective-permute-start.70) | collective-permute-done | bytes 1179680 | tf_op jit(solution)/shard_map/ppermute | solution.py:616
  876.8 8.4 maximum_select_fusion
  890.2 3.8 gather_fusion
  906.1 5.0 multiply_bitcast_fusion
  (378 shorter events, 193.1 us)
Async XLA Ops:
  7.2 27.1 %collective-permute-start.3 = (bf16[384,1152]{1,0:T(8,128)(2,1)}, bf16[384,1152]{1,0:T(8,128)(2,1)}, u32[]{:S(2)}, u32[]{:S(2)}) collective-permute-start(bf16[384,1152]{1,0:T(8,128)(2,1)} %pad_maximum_fusion.w00), channel_id=1, source_target_pairs={{0,2},{2,0},{1,3},{3,1},{4,6},{6,4},{5,7},{7,5},{8,10},{10,8},{9,1... | collective-permute-start | bytes 2654216 | tf_op jit(solution)/shard_map/ppermute | solution.py:554
  12.9 40.0 %collective-permute-start.16 = (bf16[384,1152]{1,0:T(8,128)(2,1)}, bf16[384,1152]{1,0:T(8,128)(2,1)}, u32[]{:S(2)}, u32[]{:S(2)}) collective-permute-start(bf16[384,1152]{1,0:T(8,128)(2,1)} %pad_maximum_fusion.1.w00), channel_id=1, source_target_pairs={{0,1},{1,0},{2,3},{3,2},{4,5},{5,4},{6,7},{7,6},{8,9},{9,8},{10,11... | collective-permute-start | bytes 2654216 | tf_op jit(solution)/shard_map/ppermute | solution.py:558
  42.0 77.9 %collective-permute-start.5 = (bf16[2,2,512,384]{3,2,1,0:T(8,128)(2,1)}, bf16[2,2,512,384]{3,2,1,0:T(8,128)(2,1)}, u32[]{:S(2)}, u32[]{:S(2)}) collective-permute-start(bf16[2,2,512,384]{3,2,1,0:T(8,128)(2,1)} %get-tuple-element.74.ko.vo), channel_id=1, source_target_pairs={{0,2},{2,1},{1,3},{4,6},{6,5},{5,7},{8,10},{10,9},{9,11},{12,14},{... | collective-permute-start | bytes 4718600 | tf_op jit(solution)/shard_map/ppermute | solution.py:571
  45.1 75.3 %collective-permute-start.6 = (bf16[2,2,512,384]{3,2,1,0:T(8,128)(2,1)}, bf16[2,2,512,384]{3,2,1,0:T(8,128)(2,1)}, u32[]{:S(2)}, u32[]{:S(2)}) collective-permute-start(bf16[2,2,512,384]{3,2,1,0:T(8,128)(2,1)} %get-tuple-element.74.ko.vo), channel_id=1, source_target_pairs={{2,0},{1,2},{3,1},{6,4},{5,6},{7,5},{10,8},{9,10},{11,9},{14,12},{... | collective-permute-start | bytes 4718600 | tf_op jit(solution)/shard_map/ppermute | solution.py:575
  48.4 58.8 %collective-permute-start.10 = (bf16[384,1536]{1,0:T(8,128)(2,1)}, bf16[384,1536]{1,0:T(8,128)(2,1)S(1)}, u32[]{:S(2)}, u32[]{:S(2)}) collective-permute-start(bf16[384,1536]{1,0:T(8,128)(2,1)} %get-tuple-element.150.u00), channel_id=1, source_target_pairs={{0,1},{1,0},{2,3},{3,2},{4,5},{5,4},{6,7},{7,6},{8,9},{9,8},{10,11... | collective-permute-start | bytes 3538952 | tf_op jit(solution)/shard_map/ppermute | solution.py:558
  51.6 55.6 %collective-permute-start.11 = (bf16[384,1536]{1,0:T(8,128)(2,1)}, bf16[384,1536]{1,0:T(8,128)(2,1)}, u32[]{:S(2)}, u32[]{:S(2)}) collective-permute-start(bf16[384,1536]{1,0:T(8,128)(2,1)} %get-tuple-element.150.u00), channel_id=1, source_target_pairs={{0,2},{2,0},{1,3},{3,1},{4,6},{6,4},{5,7},{7,5},{8,10},{10,8},{9,1... | collective-permute-start | bytes 3538952 | tf_op jit(solution)/shard_map/ppermute | solution.py:554
  52.9 67.0 %collective-permute-start.13 = (bf16[1536,384]{1,0:T(8,128)(2,1)}, bf16[1536,384]{1,0:T(8,128)(2,1)}, u32[]{:S(2)}, u32[]{:S(2)}) collective-permute-start(bf16[1536,384]{1,0:T(8,128)(2,1)} %get-tuple-element.148.d00), channel_id=1, source_target_pairs={{0,1},{1,0},{2,3},{3,2},{4,5},{5,4},{6,7},{7,6},{8,9},{9,8},{10,11... | collective-permute-start | bytes 3538952 | tf_op jit(solution)/shard_map/ppermute | solution.py:558
  107.2 47.5 %collective-permute-start.14 = (bf16[1536,384]{1,0:T(8,128)(2,1)}, bf16[1536,384]{1,0:T(8,128)(2,1)}, u32[]{:S(2)}, u32[]{:S(2)}) collective-permute-start(bf16[1536,384]{1,0:T(8,128)(2,1)} %get-tuple-element.148.d00), channel_id=1, source_target_pairs={{0,2},{2,0},{1,3},{3,1},{4,6},{6,4},{5,7},{7,5},{8,10},{10,8},{9,1... | collective-permute-start | bytes 3538952 | tf_op jit(solution)/shard_map/ppermute | solution.py:554
  107.2 65.7 %collective-permute-start.17 = (bf16[384,1152]{1,0:T(8,128)(2,1)}, bf16[384,1152]{1,0:T(8,128)(2,1)}, u32[]{:S(2)}, u32[]{:S(2)}) collective-permute-start(bf16[384,1152]{1,0:T(8,128)(2,1)} %pad_maximum_fusion.1.w00), channel_id=1, source_target_pairs={{0,2},{2,0},{1,3},{3,1},{4,6},{6,4},{5,7},{7,5},{8,10},{10,8},{9,1... | collective-permute-start | bytes 2654216 | tf_op jit(solution)/shard_map/ppermute | solution.py:554
  119.9 52.9 %collective-permute-start.18 = (bf16[384,1152]{1,0:T(8,128)(2,1)}, bf16[384,1152]{1,0:T(8,128)(2,1)}, u32[]{:S(2)}, u32[]{:S(2)}) collective-permute-start(bf16[384,1152]{1,0:T(8,128)(2,1)} %collective-permute-done.16.w01), channel_id=1, source_target_pairs={{0,2},{2,0},{1,3},{3,1},{4,6},{6,4},{5,7},{7,5},{8,10},{10,8},{9,1... | collective-permute-start | bytes 2654216 | tf_op jit(solution)/shard_map/ppermute | solution.py:554
  119.9 34.7 %collective-permute-start.12 = (bf16[384,1536]{1,0:T(8,128)(2,1)S(1)}, bf16[384,1536]{1,0:T(8,128)(2,1)}, u32[]{:S(2)}, u32[]{:S(2)}) collective-permute-start(bf16[384,1536]{1,0:T(8,128)(2,1)S(1)} %collective-permute-done.10.u01), channel_id=1, source_target_pairs={{0,2},{2,0},{1,3},{3,1},{4,6},{6,4},{5,7},{7,5},{8,10},{10,8},{9,1... | collective-permute-start | bytes 3538952 | tf_op jit(solution)/shard_map/ppermute | solution.py:554
  120.4 34.2 %collective-permute-start.15 = (bf16[1536,384]{1,0:T(8,128)(2,1)}, bf16[1536,384]{1,0:T(8,128)(2,1)}, u32[]{:S(2)}, u32[]{:S(2)}) collective-permute-start(bf16[1536,384]{1,0:T(8,128)(2,1)} %collective-permute-done.13.d01), channel_id=1, source_target_pairs={{0,2},{2,0},{1,3},{3,1},{4,6},{6,4},{5,7},{7,5},{8,10},{10,8},{9,1... | collective-permute-start | bytes 3538952 | tf_op jit(solution)/shard_map/ppermute | solution.py:554
  179.1 87.4 %collective-permute-start.19 = (bf16[2,2,512,384]{3,2,1,0:T(8,128)(2,1)}, bf16[2,2,512,384]{3,2,1,0:T(8,128)(2,1)}, u32[]{:S(2)}, u32[]{:S(2)}) collective-permute-start(bf16[2,2,512,384]{3,2,1,0:T(8,128)(2,1)} %get-tuple-element.80.ko.vo), channel_id=1, source_target_pairs={{0,2},{2,1},{1,3},{4,6},{6,5},{5,7},{8,10},{10,9},{9,11},{12,14},{... | collective-permute-start | bytes 4718600 | tf_op jit(solution)/shard_map/ppermute | solution.py:571
  182.6 84.0 %collective-permute-start.20 = (bf16[2,2,512,384]{3,2,1,0:T(8,128)(2,1)}, bf16[2,2,512,384]{3,2,1,0:T(8,128)(2,1)}, u32[]{:S(2)}, u32[]{:S(2)}) collective-permute-start(bf16[2,2,512,384]{3,2,1,0:T(8,128)(2,1)} %get-tuple-element.80.ko.vo), channel_id=1, source_target_pairs={{2,0},{1,2},{3,1},{6,4},{5,6},{7,5},{10,8},{9,10},{11,9},{14,12},{... | collective-permute-start | bytes 4718600 | tf_op jit(solution)/shard_map/ppermute | solution.py:575
  184.4 81.5 %collective-permute-start.24 = (bf16[384,1536]{1,0:T(8,128)(2,1)S(1)}, bf16[384,1536]{1,0:T(8,128)(2,1)}, u32[]{:S(2)}, u32[]{:S(2)}) collective-permute-start(bf16[384,1536]{1,0:T(8,128)(2,1)S(1)} %copy-done.15), channel_id=1, source_target_pairs={{0,1},{1,0},{2,3},{3,2},{4,5},{5,4},{6,7},{7,6},{8,9},{9,8},{10,11... | collective-permute-start | bytes 3538952 | tf_op jit(solution)/shard_map/ppermute | solution.py:558
  186.7 79.3 %collective-permute-start.27 = (bf16[1536,384]{1,0:T(8,128)(2,1)}, bf16[1536,384]{1,0:T(8,128)(2,1)}, u32[]{:S(2)}, u32[]{:S(2)}) collective-permute-start(bf16[1536,384]{1,0:T(8,128)(2,1)} %get-tuple-element.147.d00), channel_id=1, source_target_pairs={{0,1},{1,0},{2,3},{3,2},{4,5},{5,4},{6,7},{7,6},{8,9},{9,8},{10,11... | collective-permute-start | bytes 3538952 | tf_op jit(solution)/shard_map/ppermute | solution.py:558
  186.8 74.8 %collective-permute-start.21 = (bf16[384,384]{1,0:T(8,128)(2,1)S(1)}, bf16[384,384]{1,0:T(8,128)(2,1)S(1)}, u32[]{:S(2)}, u32[]{:S(2)}) collective-permute-start(bf16[384,384]{1,0:T(8,128)(2,1)S(1)} %copy-done.13), channel_id=1, source_target_pairs={{0,1},{1,0},{2,3},{3,2},{4,5},{5,4},{6,7},{7,6},{8,9},{9,8},{10,11... | collective-permute-start | bytes 884744 | tf_op jit(solution)/shard_map/ppermute | solution.py:558
  265.6 36.4 %collective-permute-start.25 = (bf16[384,1536]{1,0:T(8,128)(2,1)S(1)}, bf16[384,1536]{1,0:T(8,128)(2,1)}, u32[]{:S(2)}, u32[]{:S(2)}) collective-permute-start(bf16[384,1536]{1,0:T(8,128)(2,1)S(1)} %copy-done.15), channel_id=1, source_target_pairs={{0,2},{2,0},{1,3},{3,1},{4,6},{6,4},{5,7},{7,5},{8,10},{10,8},{9,1... | collective-permute-start | bytes 3538952 | tf_op jit(solution)/shard_map/ppermute | solution.py:554
  265.9 36.0 %collective-permute-start.28 = (bf16[1536,384]{1,0:T(8,128)(2,1)}, bf16[1536,384]{1,0:T(8,128)(2,1)}, u32[]{:S(2)}, u32[]{:S(2)}) collective-permute-start(bf16[1536,384]{1,0:T(8,128)(2,1)} %get-tuple-element.147.d00), channel_id=1, source_target_pairs={{0,2},{2,0},{1,3},{3,1},{4,6},{6,4},{5,7},{7,5},{8,10},{10,8},{9,1... | collective-permute-start | bytes 3538952 | tf_op jit(solution)/shard_map/ppermute | solution.py:554
  266.1 29.8 %collective-permute-start.23 = (bf16[384,384]{1,0:T(8,128)(2,1)S(1)}, bf16[384,384]{1,0:T(8,128)(2,1)S(1)}, u32[]{:S(2)}, u32[]{:S(2)}) collective-permute-start(bf16[384,384]{1,0:T(8,128)(2,1)S(1)} %collective-permute-done.21.w01), channel_id=1, source_target_pairs={{0,2},{2,0},{1,3},{3,1},{4,6},{6,4},{5,7},{7,5},{8,10},{10,8},{9,1... | collective-permute-start | bytes 884744 | tf_op jit(solution)/shard_map/ppermute | solution.py:554
  266.5 35.5 %collective-permute-start.26 = (bf16[384,1536]{1,0:T(8,128)(2,1)}, bf16[384,1536]{1,0:T(8,128)(2,1)}, u32[]{:S(2)}, u32[]{:S(2)}) collective-permute-start(bf16[384,1536]{1,0:T(8,128)(2,1)} %collective-permute-done.24.u01), channel_id=1, source_target_pairs={{0,2},{2,0},{1,3},{3,1},{4,6},{6,4},{5,7},{7,5},{8,10},{10,8},{9,1... | collective-permute-start | bytes 3538952 | tf_op jit(solution)/shard_map/ppermute | solution.py:554
  266.6 35.4 %collective-permute-start.29 = (bf16[1536,384]{1,0:T(8,128)(2,1)}, bf16[1536,384]{1,0:T(8,128)(2,1)}, u32[]{:S(2)}, u32[]{:S(2)}) collective-permute-start(bf16[1536,384]{1,0:T(8,128)(2,1)} %collective-permute-done.27.d01), channel_id=1, source_target_pairs={{0,2},{2,0},{1,3},{3,1},{4,6},{6,4},{5,7},{7,5},{8,10},{10,8},{9,1... | collective-permute-start | bytes 3538952 | tf_op jit(solution)/shard_map/ppermute | solution.py:554
  347.9 42.1 %collective-permute-start.79 = (bf16[2,9,128,128]{3,2,1,0:T(8,128)(2,1)}, bf16[2,9,128,128]{3,2,1,0:T(8,128)(2,1)}, u32[]{:S(2)}, u32[]{:S(2)}) collective-permute-start(bf16[2,9,128,128]{3,2,1,0:T(8,128)(2,1)} %get-tuple-element.132), channel_id=1, source_target_pairs={{0,2},{2,0},{1,3},{3,1},{4,6},{6,4},{5,7},{7,5},{8,10},{10,8},{9,1... | collective-permute-start | bytes 1769480 | tf_op jit(solution)/shard_map/ppermute | solution.py:554
  384.4 39.5 %collective-permute-start.32 = (bf16[2,2,512,384]{3,2,1,0:T(8,128)(2,1)}, bf16[2,2,512,384]{3,2,1,0:T(8,128)(2,1)}, u32[]{:S(2)}, u32[]{:S(2)}) collective-permute-start(bf16[2,2,512,384]{3,2,1,0:T(8,128)(2,1)} %get-tuple-element.97), channel_id=1, source_target_pairs={{0,2},{2,1},{1,3},{4,6},{6,5},{5,7},{8,10},{10,9},{9,11},{12,14},{... | collective-permute-start | bytes 4718600 | tf_op jit(solution)/shard_map/ppermute | solution.py:571
  387.9 35.9 %collective-permute-start.33 = (bf16[2,2,512,384]{3,2,1,0:T(8,128)(2,1)}, bf16[2,2,512,384]{3,2,1,0:T(8,128)(2,1)}, u32[]{:S(2)}, u32[]{:S(2)}) collective-permute-start(bf16[2,2,512,384]{3,2,1,0:T(8,128)(2,1)} %get-tuple-element.98), channel_id=1, source_target_pairs={{2,0},{1,2},{3,1},{6,4},{5,6},{7,5},{10,8},{9,10},{11,9},{14,12},{... | collective-permute-start | bytes 4718600 | tf_op jit(solution)/shard_map/ppermute | solution.py:575
  418.7 60.8 %collective-permute-start.30 = (bf16[512,384]{1,0:T(8,128)(2,1)}, bf16[512,384]{1,0:T(8,128)(2,1)}, u32[]{:S(2)}, u32[]{:S(2)}) collective-permute-start(bf16[512,384]{1,0:T(8,128)(2,1)} %get-tuple-element.158), channel_id=1, source_target_pairs={{0,2},{2,0},{1,3},{3,1},{4,6},{6,4},{5,7},{7,5},{8,10},{10,8},{9,1... | collective-permute-start | bytes 1179656 | tf_op jit(solution)/shard_map/ppermute | solution.py:554
  422.3 48.7 %collective-permute-start.82 = (bf16[288,128]{1,0:T(8,128)(2,1)}, bf16[288,128]{1,0:T(8,128)(2,1)}, u32[]{:S(2)}, u32[]{:S(2)}) collective-permute-start(bf16[288,128]{1,0:T(8,128)(2,1)} %dynamic-slice_bitcast_fusion.16), channel_id=1, source_target_pairs={{0,8},{4,12},{8,0},{12,4},{16,24},{20,28},{24,16},{28,20},{1,9},{5... | collective-permute-start | bytes 221192 | tf_op jit(solution)/shard_map/ppermute | solution.py:612
  470.4 150.2 %collective-permute-start.87 = (bf16[2,72,128,128]{3,2,1,0:T(8,128)(2,1)}, bf16[2,72,128,128]{3,2,1,0:T(8,128)(2,1)}, u32[]{:S(2)}, u32[]{:S(2)}) collective-permute-start(bf16[2,72,128,128]{3,2,1,0:T(8,128)(2,1)} %bitcast.340), channel_id=1, source_target_pairs={{0,2},{2,0},{1,3},{3,1},{4,6},{6,4},{5,7},{7,5},{8,10},{10,8},{9,1... | collective-permute-start | bytes 14155784 | tf_op jit(solution)/shard_map/ppermute | solution.py:554
  484.6 44.5 %collective-permute-start.85 = (bf16[288,128]{1,0:T(8,128)(2,1)S(1)}, bf16[288,128]{1,0:T(8,128)(2,1)S(1)}, u32[]{:S(2)}, u32[]{:S(2)}) collective-permute-start(bf16[288,128]{1,0:T(8,128)(2,1)S(1)} %maximum_select_fusion.19), channel_id=1, source_target_pairs={{0,8},{4,12},{8,0},{12,4},{16,24},{20,28},{24,16},{28,20},{1,9},{5... | collective-permute-start | bytes 221192 | tf_op jit(solution)/shard_map/ppermute | solution.py:616
  485.8 41.8 %collective-permute-start.38 = (f32[9344]{0:T(1024)S(1)}, f32[9344]{0:T(1024)S(1)}, u32[]{:S(2)}, u32[]{:S(2)}) collective-permute-start(f32[9344]{0:T(1024)S(1)} %add.355), channel_id=1, source_target_pairs={{0,1},{1,0},{2,3},{3,2},{4,5},{5,4},{6,7},{7,6},{8,9},{9,8},{10,11... | collective-permute-start | bytes 112136 | tf_op jit(solution)/shard_map/ppermute | solution.py:558
  486.9 46.8 %collective-permute-start.57 = (bf16[576,128]{1,0:T(8,128)(2,1)S(1)}, bf16[576,128]{1,0:T(8,128)(2,1)S(1)}, u32[]{:S(2)}, u32[]{:S(2)}) collective-permute-start(bf16[576,128]{1,0:T(8,128)(2,1)S(1)} %dynamic-slice_bitcast_fusion.13), channel_id=1, source_target_pairs={{0,4},{4,0},{8,12},{12,8},{16,20},{20,16},{24,28},{28,24},{1,5},{5... | collective-permute-start | bytes 442376 | tf_op jit(solution)/shard_map/ppermute | solution.py:612
  524.7 34.2 %collective-permute-start.34 = (bf16[2,2,512,384]{3,2,1,0:T(8,128)(2,1)}, bf16[2,2,512,384]{3,2,1,0:T(8,128)(2,1)}, u32[]{:S(2)}, u32[]{:S(2)}) collective-permute-start(bf16[2,2,512,384]{3,2,1,0:T(8,128)(2,1)} %get-tuple-element.112), channel_id=1, source_target_pairs={{0,2},{2,1},{1,3},{4,6},{6,5},{5,7},{8,10},{10,9},{9,11},{12,14},{... | collective-permute-start | bytes 4718600 | tf_op jit(solution)/shard_map/ppermute | solution.py:571
  527.6 33.5 %collective-permute-start.35 = (bf16[2,2,512,384]{3,2,1,0:T(8,128)(2,1)}, bf16[2,2,512,384]{3,2,1,0:T(8,128)(2,1)}, u32[]{:S(2)}, u32[]{:S(2)}) collective-permute-start(bf16[2,2,512,384]{3,2,1,0:T(8,128)(2,1)} %get-tuple-element.113), channel_id=1, source_target_pairs={{2,0},{1,2},{3,1},{6,4},{5,6},{7,5},{10,8},{9,10},{11,9},{14,12},{... | collective-permute-start | bytes 4718600 | tf_op jit(solution)/shard_map/ppermute | solution.py:575
  539.5 35.8 %collective-permute-start.71 = (bf16[2,27,128,128]{3,2,1,0:T(8,128)(2,1)}, bf16[2,27,128,128]{3,2,1,0:T(8,128)(2,1)}, u32[]{:S(2)}, u32[]{:S(2)}) collective-permute-start(bf16[2,27,128,128]{3,2,1,0:T(8,128)(2,1)} %get-tuple-element.130), channel_id=1, source_target_pairs={{0,2},{2,0},{1,3},{3,1},{4,6},{6,4},{5,7},{7,5},{8,10},{10,8},{9,1... | collective-permute-start | bytes 5308424 | tf_op jit(solution)/shard_map/ppermute | solution.py:554
  558.1 138.1 %collective-permute-start.63 = (bf16[2,72,128,128]{3,2,1,0:T(8,128)(2,1)}, bf16[2,72,128,128]{3,2,1,0:T(8,128)(2,1)}, u32[]{:S(2)}, u32[]{:S(2)}) collective-permute-start(bf16[2,72,128,128]{3,2,1,0:T(8,128)(2,1)} %bitcast.341), channel_id=1, source_target_pairs={{0,2},{2,0},{1,3},{3,1},{4,6},{6,4},{5,7},{7,5},{8,10},{10,8},{9,1... | collective-permute-start | bytes 14155784 | tf_op jit(solution)/shard_map/ppermute | solution.py:554
  576.8 27.5 %collective-permute-start.72 = (bf16[27,128,128]{2,1,0:T(8,128)(2,1)S(1)}, bf16[27,128,128]{2,1,0:T(8,128)(2,1)S(1)}, u32[]{:S(2)}, u32[]{:S(2)}) collective-permute-start(bf16[27,128,128]{2,1,0:T(8,128)(2,1)S(1)} %fusion.29), channel_id=1, source_target_pairs={{0,1},{1,0},{2,3},{3,2},{4,5},{5,4},{6,7},{7,6},{8,9},{9,8},{10,11... | collective-permute-start | bytes 2654216 | tf_op jit(solution)/shard_map/ppermute | solution.py:558
  623.8 77.0 %collective-permute-start.88 = (bf16[72,128,128]{2,1,0:T(8,128)(2,1)S(1)}, bf16[72,128,128]{2,1,0:T(8,128)(2,1)S(1)}, u32[]{:S(2)}, u32[]{:S(2)}) collective-permute-start(bf16[72,128,128]{2,1,0:T(8,128)(2,1)S(1)} %fusion), channel_id=1, source_target_pairs={{0,1},{1,0},{2,3},{3,2},{4,5},{5,4},{6,7},{7,6},{8,9},{9,8},{10,11... | collective-permute-start | bytes 7077896 | tf_op jit(solution)/shard_map/ppermute | solution.py:558
  627.4 67.6 %collective-permute-start.48 = (bf16[27,128,128]{2,1,0:T(8,128)(2,1)S(1)}, bf16[27,128,128]{2,1,0:T(8,128)(2,1)S(1)}, u32[]{:S(2)}, u32[]{:S(2)}) collective-permute-start(bf16[27,128,128]{2,1,0:T(8,128)(2,1)S(1)} %fusion.28), channel_id=1, source_target_pairs={{0,1},{1,0},{2,3},{3,2},{4,5},{5,4},{6,7},{7,6},{8,9},{9,8},{10,11... | collective-permute-start | bytes 2654216 | tf_op jit(solution)/shard_map/ppermute | solution.py:558
  640.0 68.7 %collective-permute-start.77 = (bf16[864,128]{1,0:T(8,128)(2,1)S(1)}, bf16[864,128]{1,0:T(8,128)(2,1)S(1)}, u32[]{:S(2)}, u32[]{:S(2)}) collective-permute-start(bf16[864,128]{1,0:T(8,128)(2,1)S(1)} %maximum_select_fusion.15), channel_id=1, source_target_pairs={{0,8},{4,12},{8,0},{12,4},{16,24},{20,28},{24,16},{28,20},{1,9},{5... | collective-permute-start | bytes 663560 | tf_op jit(solution)/shard_map/ppermute | solution.py:616
  698.9 51.2 %collective-permute-start.64 = (bf16[72,128,128]{2,1,0:T(8,128)(2,1)S(1)}, bf16[72,128,128]{2,1,0:T(8,128)(2,1)S(1)}, u32[]{:S(2)}, u32[]{:S(2)}) collective-permute-start(bf16[72,128,128]{2,1,0:T(8,128)(2,1)S(1)} %fusion.3), channel_id=1, source_target_pairs={{0,1},{1,0},{2,3},{3,2},{4,5},{5,4},{6,7},{7,6},{8,9},{9,8},{10,11... | collective-permute-start | bytes 7077896 | tf_op jit(solution)/shard_map/ppermute | solution.py:558
  704.0 28.9 %collective-permute-start.89 = (bf16[4608,128]{1,0:T(8,128)(2,1)S(1)}, bf16[4608,128]{1,0:T(8,128)(2,1)S(1)}, u32[]{:S(2)}, u32[]{:S(2)}) collective-permute-start(bf16[4608,128]{1,0:T(8,128)(2,1)S(1)} %dynamic-slice_bitcast_fusion), channel_id=1, source_target_pairs={{0,4},{4,0},{8,12},{12,8},{16,20},{20,16},{24,28},{28,24},{1,5},{5... | collective-permute-start | bytes 3538952 | tf_op jit(solution)/shard_map/ppermute | solution.py:612
  708.8 45.9 %collective-permute-start.78 = (bf16[1728,128]{1,0:T(8,128)(2,1)S(1)}, bf16[1728,128]{1,0:T(8,128)(2,1)S(1)}, u32[]{:S(2)}, u32[]{:S(2)}) collective-permute-start(bf16[1728,128]{1,0:T(8,128)(2,1)S(1)} %maximum_select_fusion.11), channel_id=1, source_target_pairs={{0,4},{4,0},{8,12},{12,8},{16,20},{20,16},{24,28},{28,24},{1,5},{5... | collective-permute-start | bytes 1327112 | tf_op jit(solution)/shard_map/ppermute | solution.py:616
  714.9 40.0 %collective-permute-start.51 = (bf16[432,128]{1,0:T(8,128)(2,1)S(1)}, bf16[432,128]{1,0:T(8,128)(2,1)S(1)}, u32[]{:S(2)}, u32[]{:S(2)}) collective-permute-start(bf16[432,128]{1,0:T(8,128)(2,1)S(1)} %dynamic-slice_bitcast_fusion.15), channel_id=1, source_target_pairs={{0,16},{4,20},{8,24},{12,28},{16,0},{20,4},{24,8},{28,12},{1,17},{... | collective-permute-start | bytes 331784 | tf_op jit(solution)/shard_map/ppermute | solution.py:612
  753.2 25.0 %collective-permute-start.65 = (bf16[4608,128]{1,0:T(8,128)(2,1)S(1)}, bf16[4608,128]{1,0:T(8,128)(2,1)S(1)}, u32[]{:S(2)}, u32[]{:S(2)}) collective-permute-start(bf16[4608,128]{1,0:T(8,128)(2,1)S(1)} %dynamic-slice_bitcast_fusion.1), channel_id=1, source_target_pairs={{0,4},{4,0},{8,12},{12,8},{16,20},{20,16},{24,28},{28,24},{1,5},{5... | collective-permute-start | bytes 3538952 | tf_op jit(solution)/shard_map/ppermute | solution.py:612
  755.8 25.0 %collective-permute-start.91 = (bf16[1152,128]{1,0:T(8,128)(2,1)S(1)}, bf16[1152,128]{1,0:T(8,128)(2,1)S(1)}, u32[]{:S(2)}, u32[]{:S(2)}) collective-permute-start(bf16[1152,128]{1,0:T(8,128)(2,1)S(1)} %dynamic-slice_bitcast_fusion.8), channel_id=1, source_target_pairs={{0,16},{4,20},{8,24},{12,28},{16,0},{20,4},{24,8},{28,12},{1,17},{... | collective-permute-start | bytes 884744 | tf_op jit(solution)/shard_map/ppermute | solution.py:612
  779.7 27.3 %collective-permute-start.53 = (bf16[864,128]{1,0:T(8,128)(2,1)S(1)}, bf16[864,128]{1,0:T(8,128)(2,1)S(1)}, u32[]{:S(2)}, u32[]{:S(2)}) collective-permute-start(bf16[864,128]{1,0:T(8,128)(2,1)S(1)} %maximum_select_fusion.14), channel_id=1, source_target_pairs={{0,8},{4,12},{8,0},{12,4},{16,24},{20,28},{24,16},{28,20},{1,9},{5... | collective-permute-start | bytes 663560 | tf_op jit(solution)/shard_map/ppermute | solution.py:616
  826.8 28.9 %collective-permute-start.94 = (bf16[4608,128]{1,0:T(8,128)(2,1)S(1)}, bf16[4608,128]{1,0:T(8,128)(2,1)S(1)}, u32[]{:S(2)}, u32[]{:S(2)}) collective-permute-start(bf16[4608,128]{1,0:T(8,128)(2,1)S(1)} %maximum_select_fusion.4), channel_id=1, source_target_pairs={{0,4},{4,0},{8,12},{12,8},{16,20},{20,16},{24,28},{28,24},{1,5},{5... | collective-permute-start | bytes 3538952 | tf_op jit(solution)/shard_map/ppermute | solution.py:616
  840.5 36.2 %collective-permute-start.70 = (bf16[4608,128]{1,0:T(8,128)(2,1)S(1)}, bf16[4608,128]{1,0:T(8,128)(2,1)S(1)}, u32[]{:S(2)}, u32[]{:S(2)}) collective-permute-start(bf16[4608,128]{1,0:T(8,128)(2,1)S(1)} %maximum_select_fusion.3), channel_id=1, source_target_pairs={{0,4},{4,0},{8,12},{12,8},{16,20},{20,16},{24,28},{28,24},{1,5},{5... | collective-permute-start | bytes 3538952 | tf_op jit(solution)/shard_map/ppermute | solution.py:616
  (88 other events, 2138.0 us)
